TPU v7x, 128 devices: a whole 4x4x4 slice. The times are simulated.
128 devices in a mesh: head: 8 (over y, core), row: 16 (over x, z).
Axes of the slice: x: 4, y: 4, z: 4, core: 2. Of those that a mesh axis runs over, the one named last changes fastest.
Arguments:
- hidden_in: bfloat16 [512, 2048], replicated, may hold values from -6 to 6
- w_query: bfloat16 [2048, 16, 128], P(None, 'head', 'row'), may hold values from -0.125 to 0.125
- w_key: bfloat16 [2048, 16, 128], P(None, 'head', 'row'), may hold values from -0.125 to 0.125
- w_value: bfloat16 [2048, 32, 128], P(None, 'head'), may hold values from -0.125 to 0.125
- w_zgate: bfloat16 [2048, 32, 128], P(None, 'head'), may hold values from -0.125 to 0.125
- w_decay: bfloat16 [2048, 32], P(None, 'head'), may hold values from -0.125 to 0.125
- w_beta: bfloat16 [2048, 32], P(None, 'head'), may hold values from -0.125 to 0.125
- decay_log: float32 [32], P('head'), may hold values from -1.5 to 1.5
- dt_bias: float32 [32], P('head'), may hold values from -2 to 2
- norm_gain: float32 [128], replicated, may hold values from 0.1 to 1.9
- w_out: bfloat16 [32, 128, 2048], P('head'), may hold values from -0.09375 to 0.09375
- state: float32 [512, 32, 128, 128], P(None, 'head', 'row'), may hold values from -6 to 6
Outputs:
- layer_out: bfloat16 [512, 2048], P('row', 'head')
- new_state: float32 [512, 32, 128, 128], P(None, 'head', 'row')
All inputs are finite; a program needn't handle non-finite values.
Results may differ from a plain program's by a relative error of at most 0.005.
Values sent between devices are 32-bit elements; how exact they have to be, the bound alone decides.
A program may use at most 128 MiB of HBM per device.

v0:
```python
import jax
import jax.numpy as jnp
from jax import lax
from jax.sharding import PartitionSpec as P


def split_up(value, dim, devices):
    before, after = (value.shape[:dim], value.shape[dim + 1 :])
    return jnp.moveaxis(value.reshape(*before, devices, -1, *after), dim, 0)


def summed_on_arrival(value, axis, dim):
    devices = lax.axis_size(axis)
    pieces = lax.all_to_all(split_up(value, dim, devices), axis, 0, 0, tiled=True)
    return jnp.sum(pieces, axis=0)


def local(
    hidden_in,
    w_query,
    w_key,
    w_value,
    w_zgate,
    w_decay,
    w_beta,
    decay_log,
    dt_bias,
    norm_gain,
    w_out,
    state,
):
    query = jnp.einsum("bd,dhk->bhk", hidden_in, w_query, preferred_element_type=jnp.float32)
    keys = jnp.einsum("bd,dhk->bhk", hidden_in, w_key, preferred_element_type=jnp.float32)
    values = jnp.einsum("bd,dhv->bhv", hidden_in, w_value, preferred_element_type=jnp.float32)
    decay_in = jnp.dot(hidden_in, w_decay, preferred_element_type=jnp.float32) + dt_bias
    decay = jnp.exp(-jnp.exp(decay_log) * jax.nn.softplus(decay_in))
    beta = jax.nn.sigmoid(jnp.dot(hidden_in, w_beta, preferred_element_type=jnp.float32))
    group = state.shape[1] // keys.shape[1]

    def widen(array):
        return jnp.repeat(array, group, axis=1)

    def read_state(source, vector):
        return jnp.einsum("bhkv,bhk->bhv", source, widen(vector), precision=lax.Precision.HIGHEST)

    query_sq, key_sq, raw_dot, raw_readk, raw_readq = lax.psum(
        (
            jnp.sum(query * query, axis=-1),
            jnp.sum(keys * keys, axis=-1),
            jnp.sum(query * keys, axis=-1),
            read_state(state, keys),
            read_state(state, query),
        ),
        "row",
    )
    query_scale = lax.rsqrt(1.0 + query_sq)
    key_scale = lax.rsqrt(1.0 + key_sq)
    readq_old = raw_readq * widen(query_scale)[..., None]
    unit_dot = raw_dot * query_scale * key_scale
    key_unit = keys * key_scale[..., None]
    readk = raw_readk * widen(key_scale)[..., None]
    delta = beta[..., None] * (values - decay[..., None] * readk)
    new_state = decay[..., None, None] * state + widen(key_unit)[..., None] * delta[:, :, None, :]
    own_rows = hidden_in.shape[0] // lax.axis_size("row")
    first_row = lax.axis_index("row") * own_rows
    readq_all = decay[..., None] * readq_old + widen(unit_dot)[..., None] * delta
    readq = lax.dynamic_slice_in_dim(readq_all, first_row, own_rows, 0)
    own_hidden = lax.dynamic_slice_in_dim(hidden_in, first_row, own_rows, 0)
    zgate = jnp.einsum("bd,dhv->bhv", own_hidden, w_zgate, preferred_element_type=jnp.float32)
    meansq = jnp.mean(readq * readq, axis=-1, keepdims=True)
    normed = (readq * lax.rsqrt(meansq + 0.5) * norm_gain * jax.nn.silu(zgate)).astype(jnp.bfloat16)
    partial_out = jnp.einsum("bhv,hvd->bd", normed, w_out, preferred_element_type=jnp.float32)
    layer_out = summed_on_arrival(partial_out, "head", 1).astype(jnp.bfloat16)
    return (layer_out, new_state)


def solution(mesh):
    in_specs = (
        P(),
        P(None, "head", "row"),
        P(None, "head", "row"),
        P(None, "head", None),
        P(None, "head", None),
        P(None, "head"),
        P(None, "head"),
        P("head"),
        P("head"),
        P(),
        P("head", None, None),
        P(None, "head", "row", None),
    )
    out_specs = (P("row", "head"), P(None, "head", "row", None))
    return jax.shard_map(local, mesh=mesh, in_specs=in_specs, out_specs=out_specs, check_vma=False)
```

profile of v0, /device:TPU:0, one launch (start us, length us, event | category | flops | bytes accessed | tf_op | source)
XLA Modules:
  0.0 176.4 jit_solution(13233096297192250769)
XLA Ops:
  7.2 0.0 copy-start
  7.2 0.0 all-reduce.4.cloned.1.call-start
  7.2 1.5 copy-done
  8.8 1.5 convolution_bitcast_fusion
  10.2 0.3 copy.23
  10.5 0.7 multiply_reduce_fusion.3
  11.2 0.2 copy.21
  11.4 0.4 broadcast_in_dim.15
  11.8 15.5 %fusion.45 = f32[512,4,1,128]{3,2,1,0:T(1,128)S(1)} fusion(f32[512,4,8,1]{2,3,1,0:T(1,128)S(1)} %bitcast.67, f32[512,4,8,128]{3,2,1,0:T(8,128)} %param.23), kind=kOutput, calls=%fused_computation.52 | convolution fusion | flops 25165824 | bytes 9502720 | tf_op jit(solution)/shard_map/bhkv,bhk->bhv/dot_general | solution.py:44
  27.3 0.4 broadcast_in_dim.12
  27.7 15.5 %fusion.44 = f32[512,4,1,128]{3,2,1,0:T(1,128)S(1)} fusion(f32[512,4,8,1]{2,3,1,0:T(1,128)S(1)} %bitcast.68, f32[512,4,8,128]{3,2,1,0:T(8,128)} %param.23), kind=kOutput, calls=%fused_computation.51 | convolution fusion | flops 25165824 | bytes 9502720 | tf_op jit(solution)/shard_map/bhkv,bhk->bhv/dot_general | solution.py:44
  43.2 1.5 copy_bitcast_fusion
  44.6 0.0 all-reduce.4.cloned.1.call-update
  44.6 0.0 copy-start.4
  44.7 76.2 %all-reduce = (f32[512,2]{0,1:T(2,128)S(1)}, f32[512,2]{0,1:T(2,128)S(1)}, f32[512,2]{0,1:T(2,128)S(1)}) all-reduce(f32[512,2]{0,1:T(2,128)S(1)} %get-tuple-element.4, f32[512,2]{0,1:T(2,128)S(1)} %get-tuple-element.3, f32[512,2]{0,1:T(2,128)S(1)} %get-tuple-element.2), channel_id=1, replica_groups=mesh['head'=8,'row'=16] {'row'}, use_global_device_ids=true, to_apply=%region_6.7 | all-reduce | flops 3072 | bytes 24576 | tf_op jit(solution)/shard_map/psum | solution.py:46
  121.0 0.7 fusion.39
  121.7 0.1 copy.26
  121.8 1.0 copy.27
  122.8 0.1 constant_dynamic-slice_fusion
  122.9 0.1 constant_dynamic-slice_fusion.1
  123.0 0.7 fusion.17
  123.6 15.1 %all-reduce.4.cloned.1.call-done = (f32[512,4,128]{2,0,1:T(8,128)}, f32[512,4,128]{2,0,1:T(8,128)}) async-done(((f32[512,4,128]{2,0,1:T(8,128)}, f32[512,4,128]{2,0,1:T(8,128)}), (f32[512,4,128]{2,0,1:T(8,128)}, f32[512,4,128]{2,0,1:T(8,128)})) %all-reduce.4.cloned.1.call-update) | async-done | bytes 2097168 | tf_op jit(solution)/shard_map/psum | solution.py:46
  138.8 3.1 %fusion.10 = f32[512,4,128]{2,0,1:T(8,128)S(1)} fusion(bf16[2048,4,128]{2,1,0:T(4,128)(2,1)} %param.15, bf16[512,2048]{1,0:T(8,128)(2,1)S(1)} %copy-done, f32[512,4,128]{2,0,1:T(8,128)} %get-tuple-element.8, f32[512,4]{0,1:T(4,128)S(1)} %mul.150, f32[512,4]{0,1:T(4,128)S(1)} %fusion.17, f32[512,4]{0,1:T(4,128)S(1)} %fusion.39), kind=kOutput, calls=%fused_computation.7 | convolution fusion | flops 1074790400 | bytes 6316032 | tf_op jit(solution)/shard_map/bd,dhv->bhv/dot_general | solution.py:34
  142.0 0.7 copy.28
  142.6 0.3 copy-done.1
  142.9 1.0 multiply_reduce_fusion
  144.0 3.9 %fusion.30 = f32[32,2048,1]{1,0,2:T(8,128)} fusion(bf16[4,128,2048]{2,1,0:T(8,128)(2,1)} %param.22, bf16[2048,4,128]{2,1,0:T(4,128)(2,1)} %param.16, bf16[512,2048]{1,0:T(8,128)(2,1)S(1)} %copy-done, s32[]{:T(128)S(6)} %select_n.9, f32[128]{0:T(128)S(1)} %copy-done.5, f32[32,4]{0,1:T(4,128)S(1)} %add_rsqrt_fusion.2, f32[512,4,128]{2,0,1:T(8,128)} %copy-done.1, ...), kind=kOutput, calls=%fused_computation.27 | convolution fusion | flops 134414336 | bytes 4728320 | tf_op jit(solution)/shard_map/bhv,hvd->bd/dot_general | solution.py:72
  147.9 1.7 copy.49
  149.5 4.3 %all-to-all-start = ((f32[8,32,256]{2,1,0:T(8,128)}), f32[8,32,256]{2,1,0:T(8,128)}, u32[]{:S(2)}, u32[]{:S(2)}) async-start(f32[8,32,256]{2,1,0:T(8,128)} %bitcast.70), calls=%async_computation | async-start | bytes 524288 | tf_op jit(solution)/shard_map/all_to_all | solution.py:14
  153.8 1.4 broadcast_in_dim.33
  155.2 12.7 %multiply_add_fusion = f32[512,4,8,128]{3,2,1,0:T(8,128)} fusion(f32[512,4,8,128]{3,2,1,0:T(8,128)} %param.23, f32[512,4,128]{2,1,0:T(4,128)S(1)} %copy.28, f32[512,4,8]{2,1,0:T(4,128)S(1)} %bitcast.66, f32[512,4]{1,0:T(8,128)S(1)} %copy.26), kind=kLoop, calls=%fused_computation | loop fusion | flops 6291456 | bytes 17899520 | tf_op jit(solution)/shard_map/add | solution.py:63
  167.9 1.6 reduce_sum.49
  (23 shorter events, 0.1 us)
Async XLA Ops:
  7.2 1.6 copy-start
  7.2 3.3 %copy-start.2 = (bf16[2048,2,8]{0,2,1:T(8,128)(2,1)S(1)}, bf16[2048,2,8]{0,2,1:T(8,128)(2,1)}, u32[]{:S(2)}) copy-start(bf16[2048,2,8]{0,2,1:T(8,128)(2,1)} %param.13) | copy-start | bytes 196612
  7.2 131.6 %all-reduce.4.cloned.1.call-start = ((), (), s32[]{:S(2)}) async-start(), calls=%async_computation.1 | async-start | bytes 4194304 | tf_op jit(solution)/shard_map/psum | solution.py:46
  44.6 76.3 %copy-start.7 = (f32[4]{0:T(128)S(1)}, f32[4]{0:T(128)}, u32[]{:S(2)}) copy-start(f32[4]{0:T(128)} %param.19) | copy-start | bytes 52
  44.6 76.3 %copy-start.3 = (bf16[2048,4]{0,1:T(4,128)(2,1)S(1)}, bf16[2048,4]{0,1:T(4,128)(2,1)}, u32[]{:S(2)}) copy-start(bf16[2048,4]{0,1:T(4,128)(2,1)} %param.17) | copy-start | bytes 49156
  44.6 76.3 %copy-start.6 = (f32[4]{0:T(128)S(1)}, f32[4]{0:T(128)}, u32[]{:S(2)}) copy-start(f32[4]{0:T(128)} %param.20) | copy-start | bytes 52
  44.6 78.3 %copy-start.4 = (bf16[2048,4]{0,1:T(4,128)(2,1)S(1)}, bf16[2048,4]{0,1:T(4,128)(2,1)}, u32[]{:S(2)}) copy-start(bf16[2048,4]{0,1:T(4,128)(2,1)} %param.18) | copy-start | bytes 49156
  141.9 1.0 copy-start.1
  141.9 2.0 %copy-start.5 = (f32[128]{0:T(128)S(1)}, f32[128]{0:T(128)}, u32[]{:S(2)}) copy-start(f32[128]{0:T(128)} %param.21) | copy-start | bytes 1540
  149.5 18.4 %all-to-all-start = ((f32[8,32,256]{2,1,0:T(8,128)}), f32[8,32,256]{2,1,0:T(8,128)}, u32[]{:S(2)}, u32[]{:S(2)}) async-start(f32[8,32,256]{2,1,0:T(8,128)} %bitcast.70), calls=%async_computation | async-start | bytes 524288 | tf_op jit(solution)/shard_map/all_to_all | solution.py:14
Sparse Core Ops, SparseCore 0:
  44.8 93.9 all-reduce.3
where the time goes:
time: 178 us; the launch traced here: 176 us
  blocking collectives  76.2 us (43%)
  matrix products  41.5 us (23%)
  other arithmetic  15.4 us (9%)
  waiting for transfers between devices  15.2 us (9%)
  between operations  14.3 us (8%)
  local copies, waits for them, and re-layouts  9.59 us (5%)
  starting transfers between devices  4.33 us (2%)
    psum x1, blocking collectives, local(): lax.psum((jnp.sum(query * query, axis=-1), jnp.sum(keys * keys, axis=-1),...  76.2 us
    dot_general x2, matrix products, read_state(): jnp.einsum('bhkv,bhk->bhv', source, widen(vector), precision=lax.Precisio...  31 us
    psum x1, waiting for transfers between devices, local(): lax.psum((jnp.sum(query * query, axis=-1), jnp.sum(keys * keys, axis=-1),...  15.1 us
    add x1, other arithmetic, local(): decay[..., None, None] * state  12.7 us
    all_to_all x1, starting transfers between devices, summed_on_arrival(): lax.all_to_all(split_up(value, dim, devices), axis, 0, 0, tiled=True)  4.29 us
    dot_general x1, matrix products, local(): jnp.einsum('bhv,hvd->bd', normed, w_out, preferred_element_type=jnp.float32)  3.91 us
  transfers between devices with their start and end apart: 2, of which 1 were waited for; matrix products, arithmetic and copies ran while one was open for 10% of the time, Pallas kernels for 0%

commit v1 on v0

v1 whole, which is shorter than its diff:
```python
import functools

import jax
import jax.numpy as jnp
from jax import lax
from jax.experimental import pallas as pl
from jax.experimental.pallas import tpu as pltpu
from jax.sharding import PartitionSpec as P

F32 = jnp.float32
BF16 = jnp.bfloat16
NT = (((1,), (1,)), ((), ()))
SIDE = 4
COLS = 40
HEADS = 8


def softplus(x):
    return jnp.maximum(x, 0.0) + jnp.log1p(jnp.exp(-jnp.abs(x)))


class Copies:
    def __init__(self, send, recv):
        self.send, self.recv, self.made = send, recv, []

    def start(self, src, dst, peer):
        n = len(self.made)
        copy = pltpu.make_async_remote_copy(
            src_ref=src,
            dst_ref=dst,
            send_sem=self.send.at[n],
            recv_sem=self.recv.at[n],
            device_id=peer,
            device_id_type=pl.DeviceIdType.MESH,
        )
        copy.start()
        self.made.append(copy)
        return copy


class Ring:
    def __init__(self, me, row_of):
        self.me = me
        self.right = lax.rem(me + 1, SIDE)
        self.far = lax.rem(me + 2, SIDE)
        self.left = lax.rem(me + 3, SIDE)
        self.to_right = {"row": row_of(self.right)}
        self.to_far = {"row": row_of(self.far)}
        self.to_left = {"row": row_of(self.left)}


class Scatter:
    def __init__(self, copies, ring, part, land):
        self.copies, self.ring, self.part, self.land = copies, ring, part, land

    def send_far(self):
        r = self.ring
        self.relay = [
            self.copies.start(self.part(0, r.far), self.land.at[0, 0], r.to_left),
            self.copies.start(self.part(1, r.far), self.land.at[1, 0], r.to_right),
        ]

    def send_near(self):
        r = self.ring
        self.direct = [
            self.copies.start(self.part(0, r.right), self.land.at[0, 1], r.to_right),
            self.copies.start(self.part(1, r.left), self.land.at[1, 1], r.to_left),
        ]

    def forward(self):
        r = self.ring
        self.joint = []
        for half, to, peer in ((0, r.left, r.to_left), (1, r.right, r.to_right)):
            self.relay[half].wait_recv()
            piece = self.part(half, to)
            piece[...] = piece[...] + self.land[half, 0]
            self.joint.append(self.copies.start(piece, self.land.at[half, 2], peer))

    def finish(self):
        for half in (0, 1):
            self.direct[half].wait_recv()
            self.joint[half].wait_recv()
            piece = self.part(half, self.ring.me)
            piece[...] = piece[...] + self.land[half, 1] + self.land[half, 2]


class Gather:
    def __init__(self, copies, ring, part, both):
        self.copies, self.ring, self.part, self.both = copies, ring, part, both

    def send(self):
        r = self.ring
        mine = self.both(r.me)
        self.near = [
            self.copies.start(mine, mine, r.to_right),
            self.copies.start(mine, mine, r.to_left),
        ]

    def forward(self):
        r = self.ring
        self.far = []
        for n, (half, at, peer) in enumerate(((0, r.left, r.to_right), (1, r.right, r.to_left))):
            self.near[n].wait_recv()
            piece = self.part(half, at)
            self.far.append(self.copies.start(piece, piece, peer))

    def finish(self):
        for copy in self.far:
            copy.wait_recv()


def exchange_kernel(
    hid,
    wq,
    wk,
    wd,
    wb,
    values,
    zgate,
    decay_log,
    dt_bias,
    gain,
    w_out,
    state,
    delta_all,
    proj,
    layer_out,
    held,
    spread,
    part,
    land1,
    land2,
    small,
    small_land1,
    small_land2,
    scales,
    normed,
    outs,
    outs_land,
    load_sem,
    send_sem,
    recv_sem,
):
    row = lax.axis_index("row")
    head = lax.axis_index("head")
    x, z = row // SIDE, lax.rem(row, SIDE)
    blk = held.shape[0] // (SIDE * SIDE)

    barrier = pltpu.get_barrier_semaphore()
    peers = []
    for d in (1, 2, 3):
        peers.append({"row": lax.rem(x + d, SIDE) * SIDE + z})
        peers.append({"row": x * SIDE + lax.rem(z + d, SIDE)})
    for d in range(1, HEADS):
        peers.append({"head": lax.rem(head + d, HEADS)})
    for peer in peers:
        pl.semaphore_signal(barrier, inc=1, device_id=peer, device_id_type=pl.DeviceIdType.MESH)

    def row_at(o, first, second):
        return first * SIDE + second if o == 0 else second * SIDE + first

    rings1 = [
        Ring(x, lambda a: row_at(0, a, z)),
        Ring(z, lambda a: row_at(1, a, x)),
    ]
    rings2 = [
        Ring(z, lambda b: row_at(0, x, b)),
        Ring(x, lambda b: row_at(1, z, b)),
    ]
    order = [[r.far, r.right, r.left, r.me] for r in rings1]

    loads = {}
    for j in range(SIDE):
        for o in (0, 1):
            for b in range(SIDE):
                n = (j * 2 + o) * SIDE + b
                at = row_at(o, order[o][j], b) * blk
                loads[j, o, b] = pltpu.make_async_copy(
                    state.at[pl.ds(at, blk), pl.ds(2 * o, 2)],
                    held.at[pl.ds(at, blk), pl.ds(2 * o, 2)],
                    load_sem.at[n],
                )
                loads[j, o, b].start()

    w = jnp.concatenate(
        [wq[0].astype(F32), wq[1].astype(F32), wk[0].astype(F32), wk[1].astype(F32), wd[...].astype(F32), wb[...].astype(F32)],
        axis=0,
    ).astype(BF16)
    proj[...] = lax.dot_general(hid[...], w, NT, preferred_element_type=F32)

    col = lax.broadcasted_iota(jnp.int32, (COLS, 512), 0)
    lane = lax.broadcasted_iota(jnp.int32, (COLS, 512), 1)
    for hk in (0, 1):
        base = jnp.where(lane < 256, 16, 0) + 8 * hk
        spread[hk] = (col == base + lane % 8).astype(F32).astype(BF16)

    q, k = proj[:, 0:16], proj[:, 16:32]
    seg = (
        lax.broadcasted_iota(jnp.int32, (8, 16), 1) // 8 == lax.broadcasted_iota(jnp.int32, (8, 16), 0)
    ).astype(F32)
    seg_k = (
        lax.broadcasted_iota(jnp.int32, (8, 16), 1) // 8 + 2 == lax.broadcasted_iota(jnp.int32, (8, 16), 0)
    ).astype(F32)
    seg_qk = (
        lax.broadcasted_iota(jnp.int32, (8, 16), 1) // 8 + 4 == lax.broadcasted_iota(jnp.int32, (8, 16), 0)
    ).astype(F32)
    sums = (
        lax.dot_general(seg, q * q, NT, precision=lax.Precision.HIGHEST, preferred_element_type=F32)
        + lax.dot_general(seg_k, k * k, NT, precision=lax.Precision.HIGHEST, preferred_element_type=F32)
        + lax.dot_general(seg_qk, q * k, NT, precision=lax.Precision.HIGHEST, preferred_element_type=F32)
    )
    for a in range(SIDE):
        small[a] = sums[:, a * 128 : (a + 1) * 128]

    pl.semaphore_wait(barrier, len(peers))
    copies = Copies(send_sem, recv_sem)

    small1 = []
    for d in (1, 2, 3):
        to = lax.rem(x + d, SIDE)
        small1.append(copies.start(small.at[to], small_land1.at[d - 1], {"row": to * SIDE + z}))

    own_lane = lax.broadcasted_iota(jnp.int32, (2 * blk, 8 * blk), 1) // 8
    own_row = lax.rem(lax.broadcasted_iota(jnp.int32, (2 * blk, 8 * blk), 0), blk)
    own = own_lane == own_row

    def read_block(o, first, second):
        at = pl.multiple_of(row_at(o, first, second) * blk, blk)
        vec = proj[pl.ds(at, blk), :].astype(BF16)
        wide = jnp.dot(vec, spread[o], preferred_element_type=F32)
        wide = jnp.concatenate([wide[:, : 8 * blk], wide[:, 8 * blk :]], axis=0)
        wide = jnp.where(own, wide, 0.0).astype(BF16)
        block = jnp.concatenate(
            [held[pl.ds(at, blk), 2 * o + c].reshape(8 * blk, 128).astype(BF16) for c in (0, 1)], axis=1
        )
        read = jnp.dot(wide, block, preferred_element_type=F32)
        for c in (0, 1):
            for t in (0, 1):
                part[o, c, t, first, second] = read[t * blk : (t + 1) * blk, c * 128 : (c + 1) * 128]

    def scatter1(o, t):
        return Scatter(copies, rings1[o], lambda c, a: part.at[o, c, t, a], land1.at[o, t])

    def scatter2(o, t):
        return Scatter(copies, rings2[o], lambda c, b: part.at[o, c, t, rings1[o].me, b], land2.at[o, t])

    k1 = [scatter1(o, 0) for o in (0, 1)]
    q1 = [scatter1(o, 1) for o in (0, 1)]
    k2 = [scatter2(o, 0) for o in (0, 1)]
    q2 = [scatter2(o, 1) for o in (0, 1)]

    for j in range(SIDE):
        for o in (0, 1):
            for b in range(SIDE):
                loads[j, o, b].wait()
                read_block(o, order[o][j], b)
            if j == 0:
                k1[o].send_far()
            if j == 2:
                k1[o].send_near()

    for s in q1:
        s.send_far()

    for copy in small1:
        copy.wait_recv()
    small[x] = small[x] + small_land1[0] + small_land1[1] + small_land1[2]
    small2 = []
    for d in (1, 2, 3):
        to = lax.rem(z + d, SIDE)
        small2.append(copies.start(small.at[x], small_land2.at[d - 1], {"row": x * SIDE + to}))

    for s in k1:
        s.forward()
    for s in q1:
        s.send_near()
    for s in q1:
        s.forward()
    for s in k1:
        s.finish()
    for s in k2:
        s.send_far()
        s.send_near()

    for copy in small2:
        copy.wait_recv()
    total = small[x] + small_land2[0] + small_land2[1] + small_land2[2]
    scales[...] = jnp.concatenate([total, jnp.zeros((120, 128), F32)], axis=0).T
    mine = pl.ds(pl.multiple_of(row * blk, blk), blk)
    raw = scales[pl.ds(pl.multiple_of(z * blk, blk), blk), :]
    own_proj = proj[mine, :]
    q_scale = lax.rsqrt(1.0 + raw[:, 0:2])
    k_scale = lax.rsqrt(1.0 + raw[:, 2:4])
    unit_dot = raw[:, 4:6] * q_scale * k_scale
    decay = jnp.exp(-jnp.exp(decay_log[...]) * softplus(own_proj[:, 32:36] + dt_bias[...]))
    beta = 1.0 / (1.0 + jnp.exp(-own_proj[:, 36:40]))

    for s in k2:
        s.forward()
    for s in k2:
        s.finish()

    deltas = []
    for h in range(4):
        o, c = h // 2, h % 2
        r1, r2 = rings1[o], rings2[o]
        readk = part[o, c, 0, r1.me, r2.me] * k_scale[:, o : o + 1]
        delta = beta[:, h : h + 1] * (values[:, h * 128 : (h + 1) * 128] - decay[:, h : h + 1] * readk)
        delta_all[o, c, r1.me, r2.me] = delta * k_scale[:, o : o + 1]
        deltas.append(delta)

    g2 = [
        Gather(
            copies,
            rings2[o],
            lambda c, b, o=o: delta_all.at[o, c, rings1[o].me, b],
            lambda b, o=o: delta_all.at[o, :, rings1[o].me, b],
        )
        for o in (0, 1)
    ]
    g1 = [
        Gather(
            copies,
            rings1[o],
            lambda c, a, o=o: delta_all.at[o, c, a],
            lambda a, o=o: delta_all.at[o, :, a],
        )
        for o in (0, 1)
    ]
    for g in g2:
        g.send()
    for s in q1:
        s.finish()
    for s in q2:
        s.send_far()
        s.send_near()
    for g in g2:
        g.forward()
    for s in q2:
        s.forward()
    for g in g2:
        g.finish()
    for g in g1:
        g.send()
    for s in q2:
        s.finish()

    for h in range(4):
        o, c = h // 2, h % 2
        r1, r2 = rings1[o], rings2[o]
        old = part[o, c, 1, r1.me, r2.me] * q_scale[:, o : o + 1]
        readq = decay[:, h : h + 1] * old + unit_dot[:, o : o + 1] * deltas[h]
        meansq = jnp.mean(readq * readq, axis=-1, keepdims=True)
        gate = zgate[:, h * 128 : (h + 1) * 128]
        gate = gate / (1.0 + jnp.exp(-gate))
        normed[:, h * 128 : (h + 1) * 128] = (readq * lax.rsqrt(meansq + 0.5) * gain[...] * gate).astype(BF16)

    width = outs.shape[-1]
    for n in range(HEADS):
        outs[n] = jnp.dot(normed[...], w_out[:, n * width : (n + 1) * width], preferred_element_type=F32)
    out_copies = []
    for d in range(1, HEADS):
        to = lax.rem(head + d, HEADS)
        out_copies.append(copies.start(outs.at[to], outs_land.at[head], {"head": to}))
    outs_land[head] = outs[head]

    for g in g1:
        g.forward()
    for copy in out_copies:
        copy.wait_recv()
    total_out = outs_land[0]
    for n in range(1, HEADS):
        total_out = total_out + outs_land[n]
    layer_out[...] = total_out.astype(BF16)
    for g in g1:
        g.finish()
    for copy in copies.made:
        copy.wait_send()


def update_kernel(decay_log, dt_bias, proj, delta_all, state, new_state):
    r = pl.program_id(0)
    a, b = r // SIDE, lax.rem(r, SIDE)
    blk = state.shape[0]
    vec = proj[...]
    decay = jnp.exp(-jnp.exp(decay_log[...]) * softplus(vec[:, 32:36] + dt_bias[...]))
    hi = vec.astype(BF16)
    lo = (vec - hi.astype(F32)).astype(BF16)
    three = jnp.concatenate([hi.astype(F32), hi.astype(F32), lo.astype(F32)], axis=0).astype(BF16)
    own = (
        lax.broadcasted_iota(jnp.int32, (8 * blk, 3 * blk), 0) // 8
        == lax.rem(lax.broadcasted_iota(jnp.int32, (8 * blk, 3 * blk), 1), blk)
    )
    for o in (0, 1):
        pick = (
            lax.broadcasted_iota(jnp.int32, (8 * blk, COLS), 1)
            == 16 + 8 * o + lax.rem(lax.broadcasted_iota(jnp.int32, (8 * blk, COLS), 0), 8)
        ).astype(F32).astype(BF16)
        wide = lax.dot_general(pick, three, NT, preferred_element_type=F32)
        wide = jnp.where(own, wide, 0.0).astype(BF16)
        first, second = (a, b) if o == 0 else (b, a)
        step = jnp.concatenate([delta_all[o, c, first, second] for c in (0, 1)], axis=1)
        step_hi = step.astype(BF16)
        step_lo = (step - step_hi.astype(F32)).astype(BF16)
        steps = jnp.concatenate([step_hi, step_lo, step_hi], axis=0)
        add = jnp.dot(wide, steps, preferred_element_type=F32)
        for c in (0, 1):
            h = 2 * o + c
            keep = jnp.broadcast_to(decay[:, h : h + 1], (blk, 128))
            new_state[:, h] = keep[:, None, :] * state[:, h] + add[:, c * 128 : (c + 1) * 128].reshape(blk, 8, 128)


def local(
    hidden_in,
    w_query,
    w_key,
    w_value,
    w_zgate,
    w_decay,
    w_beta,
    decay_log,
    dt_bias,
    norm_gain,
    w_out,
    state,
):
    seqs, width = hidden_in.shape
    rows = SIDE * SIDE
    blk = seqs // rows
    first_row = lax.axis_index("row") * blk
    own_hidden = lax.dynamic_slice_in_dim(hidden_in, first_row, blk, 0)
    values = jnp.einsum("bd,dhv->bhv", own_hidden, w_value, preferred_element_type=F32).reshape(blk, 512)
    zgate = jnp.einsum("bd,dhv->bhv", own_hidden, w_zgate, preferred_element_type=F32).reshape(blk, 512)
    vmem = pl.BlockSpec(memory_space=pltpu.VMEM)
    n_copies = 3 + 3 + 2 * 2 * 6 * 2 + 2 * 2 * 4 + HEADS - 1
    delta_all, proj, layer_out = pl.pallas_call(
        exchange_kernel,
        out_shape=(
            jax.ShapeDtypeStruct((2, 2, SIDE, SIDE, blk, 128), F32),
            jax.ShapeDtypeStruct((seqs, COLS), F32),
            jax.ShapeDtypeStruct((blk, 256), BF16),
        ),
        in_specs=[vmem] * 11 + [pl.BlockSpec(memory_space=pl.ANY)],
        out_specs=(vmem, vmem, vmem),
        scratch_shapes=[
            pltpu.VMEM((seqs, 4, 8, 128), F32),
            pltpu.VMEM((2, COLS, 512), BF16),
            pltpu.VMEM((2, 2, 2, SIDE, SIDE, blk, 128), F32),
            pltpu.VMEM((2, 2, 2, 3, SIDE, blk, 128), F32),
            pltpu.VMEM((2, 2, 2, 3, blk, 128), F32),
            pltpu.VMEM((SIDE, 8, 128), F32),
            pltpu.VMEM((3, 8, 128), F32),
            pltpu.VMEM((3, 8, 128), F32),
            pltpu.VMEM((128, 128), F32),
            pltpu.VMEM((blk, 512), BF16),
            pltpu.VMEM((HEADS, blk, 256), F32),
            pltpu.VMEM((HEADS, blk, 256), F32),
            pltpu.SemaphoreType.DMA((32,)),
            pltpu.SemaphoreType.DMA((n_copies,)),
            pltpu.SemaphoreType.DMA((n_copies,)),
        ],
        compiler_params=pltpu.CompilerParams(
            collective_id=0, has_side_effects=True, vmem_limit_bytes=48 * 1024 * 1024
        ),
        name="exchange",
    )(
        hidden_in,
        jnp.transpose(w_query, (1, 2, 0)),
        jnp.transpose(w_key, (1, 2, 0)),
        jnp.transpose(w_decay, (1, 0)),
        jnp.transpose(w_beta, (1, 0)),
        values,
        zgate,
        decay_log.reshape(1, 4),
        dt_bias.reshape(1, 4),
        norm_gain.reshape(1, 128),
        w_out.reshape(512, width),
        state,
    )
    new_state = pl.pallas_call(
        update_kernel,
        grid=(rows,),
        out_shape=jax.ShapeDtypeStruct(state.shape, F32),
        in_specs=[
            pl.BlockSpec((1, 4), lambda r: (0, 0)),
            pl.BlockSpec((1, 4), lambda r: (0, 0)),
            pl.BlockSpec((blk, COLS), lambda r: (r, 0)),
            pl.BlockSpec((2, 2, SIDE, SIDE, blk, 128), lambda r: (0, 0, 0, 0, 0, 0)),
            pl.BlockSpec((blk, 4, 8, 128), lambda r: (r, 0, 0, 0)),
        ],
        out_specs=pl.BlockSpec((blk, 4, 8, 128), lambda r: (r, 0, 0, 0)),
        name="update",
    )(decay_log.reshape(1, 4), dt_bias.reshape(1, 4), proj, delta_all, state)
    return (layer_out, new_state)


def solution(mesh):
    in_specs = (
        P(),
        P(None, "head", "row"),
        P(None, "head", "row"),
        P(None, "head", None),
        P(None, "head", None),
        P(None, "head"),
        P(None, "head"),
        P("head"),
        P("head"),
        P(),
        P("head", None, None),
        P(None, "head", "row", None),
    )
    out_specs = (P("row", "head"), P(None, "head", "row", None))
    return jax.shard_map(local, mesh=mesh, in_specs=in_specs, out_specs=out_specs, check_vma=False)
```

time: 178 us -> 69.2 us (0.39)
  blocking collectives: 76.2 us -> 0 us
  Pallas kernels: 0 us -> 60.4 us
  matrix products: 41.5 us -> 3.58 us
  other arithmetic: 15.4 us -> 0 us
  waiting for transfers between devices: 15.2 us -> 0 us
  between operations: 14.3 us -> 0.78 us
  local copies, waits for them, and re-layouts: 9.59 us -> 3.92 us
  starting transfers between devices: 4.33 us -> 0 us
    psum x1 -> x0, blocking collectives: 76.2 us -> none  [local(): lax.psum((jnp.sum(query * query, axis=-1), jnp.sum(keys * keys, axis=-1),...]
    pallas_call x0 -> x2, Pallas kernels: none -> 60.4 us  [the longest x1 44.7 us: local(): pl.pallas_call(exchange_kernel, out_shape=(jax.ShapeDtypeStruct((2, 2, SI...]
    dot_general x6 -> x2, matrix products: 39.4 us -> 3.58 us  [the longest x1 2.06 us: local(): jnp.einsum('bd,dhv->bhv', own_hidden, w_zgate, preferred_element_type=F32)]
    psum x1 -> x0, waiting for transfers between devices: 15.1 us -> none  [local(): lax.psum((jnp.sum(query * query, axis=-1), jnp.sum(keys * keys, axis=-1),...]
    add x1 -> x0, other arithmetic: 12.7 us -> none  [local(): decay[..., None, None] * state]
    all_to_all x1 -> x0, starting transfers between devices: 4.29 us -> none  [summed_on_arrival(): lax.all_to_all(split_up(value, dim, devices), axis, 0, 0, tiled=True)]
    reduce_sum x2 -> x0, other arithmetic: 2.61 us -> none  [the longest x1 1.58 us: summed_on_arrival(): return jnp.sum(pieces, axis=0)]
    unnamed x2 -> x0, matrix products: 2.16 us -> none
  transfers between devices with their start and end apart: 2 -> 0, of which waited for: 1 -> 0; matrix products, arithmetic and copies ran while one was open for 10% -> 0% of each run, Pallas kernels for 0% -> 0%
where the time goes in v1:
time: 69.2 us; the launch traced here: 68.7 us
  Pallas kernels  60.4 us (87%)
  local copies, waits for them, and re-layouts  3.92 us (6%)
  matrix products  3.58 us (5%)
  between operations  0.78 us (1%)
    pallas_call x1, Pallas kernels, local(): pl.pallas_call(exchange_kernel, out_shape=(jax.ShapeDtypeStruct((2, 2, SI...  44.7 us
    pallas_call x1, Pallas kernels, local(): pl.pallas_call(update_kernel, grid=(rows,), out_shape=jax.ShapeDtypeStruc...  15.7 us
    unnamed x25, local copies, waits for them, and re-layouts  3.9 us
    dot_general x1, matrix products, local(): jnp.einsum('bd,dhv->bhv', own_hidden, w_zgate, preferred_element_type=F32)  2.06 us
    dot_general x1, matrix products, local(): jnp.einsum('bd,dhv->bhv', own_hidden, w_value, preferred_element_type=F32)  1.52 us

profile of v1, /device:TPU:0, one launch (start us, length us, event | category | flops | bytes accessed | tf_op | source)
XLA Modules:
  0.0 68.7 jit_solution(16842535096376401155)
XLA Ops:
  0.6 0.0 copy-start
  0.7 0.0 copy-start.1
  0.7 1.6 %copy-done = bf16[2048,4,128]{2,1,0:T(4,128)(2,1)S(1)} copy-done((bf16[2048,4,128]{2,1,0:T(4,128)(2,1)S(1)}, bf16[2048,4,128]{2,1,0:T(4,128)(2,1)}, u32[]{:S(2)}) %copy-start) | copy-done | bytes 2097176
  2.2 0.0 copy-start.2
  2.2 0.0 copy-start.5
  2.2 0.0 copy-start.6
  2.2 0.0 copy-start.7
  2.2 0.0 copy-start.8
  2.3 0.0 copy-start.9
  2.3 0.0 copy-start.10
  2.3 0.0 copy-start.11
  2.3 1.5 %fusion.4 = f32[4,4,8,128]{3,2,1,0:T(8,128)S(1)} fusion(bf16[2048,4,128]{2,1,0:T(4,128)(2,1)S(1)} %copy-done, bf16[512,2048]{1,0:T(8,128)(2,1)} %hid.1, s32[]{:T(128)S(6)} %select_n.3), kind=kOutput, calls=%fused_computation.4 | convolution fusion | flops 67108864 | bytes 2293764 | tf_op jit(solution)/shard_map/bd,dhv->bhv/dot_general | solution.py:432
  3.8 0.0 copy-done.1
  3.8 2.1 %fusion.7 = f32[4,4,8,128]{3,2,1,0:T(8,128)S(1)} fusion(bf16[2048,4,128]{2,1,0:T(4,128)(2,1)} %param.16, bf16[512,2048]{1,0:T(8,128)(2,1)S(1)} %copy-done.1, s32[]{:T(128)S(6)} %select_n.3), kind=kOutput, calls=%fused_computation.5 | convolution fusion | flops 67108864 | bytes 2293764 | tf_op jit(solution)/shard_map/bd,dhv->bhv/dot_general | solution.py:433
  5.9 0.0 copy-done.2
  5.9 0.0 copy-done.5
  5.9 0.0 copy-done.6
  5.9 0.0 copy-done.7
  5.9 0.0 copy-done.8
  5.9 0.0 copy-done.9
  6.0 0.0 copy-done.10
  6.0 0.0 copy-done.11
  6.0 44.7 %exchange.1 = (f32[2,2,4,4,32,128]{5,4,3,2,1,0:T(8,128)S(1)}, f32[512,40]{1,0:T(8,128)S(1)}, bf16[32,256]{1,0:T(8,128)(2,1)S(1)}) custom-call(bf16[512,2048]{1,0:T(8,128)(2,1)S(1)} %copy-done.1, bf16[2,8,2048]{2,1,0:T(8,128)(2,1)S(1)} %bitcast.22, bf16[2,8,2048]{2,1,0:T(8,128)(2,1)S(1)} %bitcast.23, bf16[4,2048]{1,0:T(4,128)(2,1)S(1)} %bitcast.24, ...), custom_call_target="tpu_custom_call" | custom-call | tf_op jit(solution)/shard_map/exchange/pallas_call | solution.py:436
  50.7 0.0 copy-start.3
  50.7 1.0 %copy-done.3 = f32[2,2,4,4,32,128]{5,4,3,2,1,0:T(8,128)} copy-done((f32[2,2,4,4,32,128]{5,4,3,2,1,0:T(8,128)}, f32[2,2,4,4,32,128]{5,4,3,2,1,0:T(8,128)S(1)}, u32[]{:S(2)}) %copy-start.3) | copy-done | bytes 1048600
  51.6 0.0 copy-start.4
  51.6 0.7 %copy-done.4 = f32[512,40]{1,0:T(8,128)} copy-done((f32[512,40]{1,0:T(8,128)}, f32[512,40]{1,0:T(8,128)S(1)}, u32[]{:S(2)}) %copy-start.4) | copy-done | bytes 81944
  52.4 15.7 %update.1 = f32[512,4,8,128]{3,2,1,0:T(8,128)} custom-call(f32[1,4]{1,0:T(1,128)} %bitcast.26, f32[1,4]{1,0:T(1,128)} %bitcast.28, f32[512,40]{1,0:T(8,128)} %copy-done.4, f32[2,2,4,4,32,128]{5,4,3,2,1,0:T(8,128)} %copy-done.3, f32[512,4,8,128]{3,2,1,0:T(8,128)} %state.3), custom_call_target="tpu_custom_call" | custom-call | tf_op jit(solution)/shard_map/update/pallas_call | solution.py:480
  68.1 0.6 copy.31
  (1 shorter events, 0.0 us)
Async XLA Ops:
  0.6 1.6 %copy-start = (bf16[2048,4,128]{2,1,0:T(4,128)(2,1)S(1)}, bf16[2048,4,128]{2,1,0:T(4,128)(2,1)}, u32[]{:S(2)}) copy-start(bf16[2048,4,128]{2,1,0:T(4,128)(2,1)} %param.15) | copy-start | bytes 6291460
  0.7 3.2 %copy-start.1 = (bf16[512,2048]{1,0:T(8,128)(2,1)S(1)}, bf16[512,2048]{1,0:T(8,128)(2,1)}, u32[]{:S(2)}) copy-start(bf16[512,2048]{1,0:T(8,128)(2,1)} %hid.1) | copy-start | bytes 6291460
  2.2 3.7 %copy-start.2 = (bf16[4,128,2048]{2,1,0:T(8,128)(2,1)S(1)}, bf16[4,128,2048]{2,1,0:T(8,128)(2,1)}, u32[]{:S(2)}) copy-start(bf16[4,128,2048]{2,1,0:T(8,128)(2,1)} %param.22) | copy-start | bytes 6291460
  2.2 3.7 %copy-start.5 = (bf16[2048,2,8]{0,2,1:T(8,128)(2,1)S(1)}, bf16[2048,2,8]{0,2,1:T(8,128)(2,1)}, u32[]{:S(2)}) copy-start(bf16[2048,2,8]{0,2,1:T(8,128)(2,1)} %param.13) | copy-start | bytes 196612
  2.2 3.7 %copy-start.6 = (bf16[2048,2,8]{0,2,1:T(8,128)(2,1)S(1)}, bf16[2048,2,8]{0,2,1:T(8,128)(2,1)}, u32[]{:S(2)}) copy-start(bf16[2048,2,8]{0,2,1:T(8,128)(2,1)} %param.14) | copy-start | bytes 196612
  2.2 3.7 %copy-start.7 = (bf16[2048,4]{0,1:T(4,128)(2,1)S(1)}, bf16[2048,4]{0,1:T(4,128)(2,1)}, u32[]{:S(2)}) copy-start(bf16[2048,4]{0,1:T(4,128)(2,1)} %param.17) | copy-start | bytes 49156
  2.2 3.7 %copy-start.8 = (bf16[2048,4]{0,1:T(4,128)(2,1)S(1)}, bf16[2048,4]{0,1:T(4,128)(2,1)}, u32[]{:S(2)}) copy-start(bf16[2048,4]{0,1:T(4,128)(2,1)} %param.18) | copy-start | bytes 49156
  2.3 3.7 %copy-start.9 = (f32[4]{0:T(128)S(1)}, f32[4]{0:T(128)}, u32[]{:S(2)}) copy-start(f32[4]{0:T(128)} %param.19) | copy-start | bytes 52
  2.3 3.7 %copy-start.10 = (f32[4]{0:T(128)S(1)}, f32[4]{0:T(128)}, u32[]{:S(2)}) copy-start(f32[4]{0:T(128)} %param.20) | copy-start | bytes 52
  2.3 3.7 %copy-start.11 = (f32[128]{0:T(128)S(1)}, f32[128]{0:T(128)}, u32[]{:S(2)}) copy-start(f32[128]{0:T(128)} %param.21) | copy-start | bytes 1540
  50.7 1.0 %copy-start.3 = (f32[2,2,4,4,32,128]{5,4,3,2,1,0:T(8,128)}, f32[2,2,4,4,32,128]{5,4,3,2,1,0:T(8,128)S(1)}, u32[]{:S(2)}) copy-start(f32[2,2,4,4,32,128]{5,4,3,2,1,0:T(8,128)S(1)} %get-tuple-element.7.delta_all) | copy-start | bytes 3145732
  51.6 0.7 %copy-start.4 = (f32[512,40]{1,0:T(8,128)}, f32[512,40]{1,0:T(8,128)S(1)}, u32[]{:S(2)}) copy-start(f32[512,40]{1,0:T(8,128)S(1)} %get-tuple-element.6.proj) | copy-start | bytes 245764

commit v2 on v1

v2 whole, which is shorter than its diff:
```python
import functools

import jax
import jax.numpy as jnp
from jax import lax
from jax.experimental import pallas as pl
from jax.experimental.pallas import tpu as pltpu
from jax.sharding import PartitionSpec as P

F32 = jnp.float32
BF16 = jnp.bfloat16
NT = (((1,), (1,)), ((), ()))
SIDE = 4
COLS = 40
HEADS = 8


def softplus(x):
    return jnp.maximum(x, 0.0) + jnp.log1p(jnp.exp(-jnp.abs(x)))


class Copies:
    def __init__(self, send, recv):
        self.send, self.recv, self.made = send, recv, []

    def start(self, src, dst, peer):
        n = len(self.made)
        copy = pltpu.make_async_remote_copy(
            src_ref=src,
            dst_ref=dst,
            send_sem=self.send.at[n],
            recv_sem=self.recv.at[n],
            device_id=peer,
            device_id_type=pl.DeviceIdType.MESH,
        )
        copy.start()
        self.made.append(copy)
        return copy


class Ring:
    def __init__(self, me, row_of):
        self.me = me
        self.right = lax.rem(me + 1, SIDE)
        self.far = lax.rem(me + 2, SIDE)
        self.left = lax.rem(me + 3, SIDE)
        self.to_right = {"row": row_of(self.right)}
        self.to_far = {"row": row_of(self.far)}
        self.to_left = {"row": row_of(self.left)}


class Scatter:
    def __init__(self, copies, ring, part, land):
        self.copies, self.ring, self.part, self.land = copies, ring, part, land

    def send_far(self):
        r = self.ring
        self.relay = [
            self.copies.start(self.part(0, r.far), self.land.at[0, 0], r.to_left),
            self.copies.start(self.part(1, r.far), self.land.at[1, 0], r.to_right),
        ]

    def send_near(self):
        r = self.ring
        self.direct = [
            self.copies.start(self.part(0, r.right), self.land.at[0, 1], r.to_right),
            self.copies.start(self.part(1, r.left), self.land.at[1, 1], r.to_left),
        ]

    def forward(self):
        r = self.ring
        self.joint = []
        for half, to, peer in ((0, r.left, r.to_left), (1, r.right, r.to_right)):
            self.relay[half].wait_recv()
            piece = self.part(half, to)
            piece[...] = piece[...] + self.land[half, 0]
            self.joint.append(self.copies.start(piece, self.land.at[half, 2], peer))

    def finish(self):
        for half in (0, 1):
            self.direct[half].wait_recv()
            self.joint[half].wait_recv()
            piece = self.part(half, self.ring.me)
            piece[...] = piece[...] + self.land[half, 1] + self.land[half, 2]


class Direct:
    def __init__(self, copies, ring):
        self.copies, self.ring, self.sent = copies, ring, []

    def send(self, src, dst):
        r = self.ring
        for d, (at, peer) in enumerate(((r.right, r.to_right), (r.left, r.to_left), (r.far, r.to_far))):
            self.sent.append(self.copies.start(src(at), dst(d), peer))

    def wait(self):
        for copy in self.sent:
            copy.wait_recv()


class Gather:
    def __init__(self, copies, ring, part, both):
        self.copies, self.ring, self.part, self.both = copies, ring, part, both

    def send(self):
        r = self.ring
        mine = self.both(r.me)
        self.near = [
            self.copies.start(mine, mine, r.to_right),
            self.copies.start(mine, mine, r.to_left),
        ]

    def forward(self):
        r = self.ring
        self.far = []
        for n, (half, at, peer) in enumerate(((0, r.left, r.to_right), (1, r.right, r.to_left))):
            self.near[n].wait_recv()
            piece = self.part(half, at)
            self.far.append(self.copies.start(piece, piece, peer))

    def finish(self):
        for copy in self.far:
            copy.wait_recv()


def split(x):
    hi = x.astype(BF16)
    return hi, (x - hi.astype(F32)).astype(BF16)


def exchange_kernel(
    wq,
    wk,
    wd,
    wb,
    decay_log,
    dt_bias,
    gain,
    hid_hbm,
    wv_hbm,
    wz_hbm,
    w_out_hbm,
    state,
    layer_out,
    held,
    hid,
    wv,
    wz,
    w_out,
    proj,
    decay_all,
    spread,
    part,
    land1,
    land2,
    delta_all,
    lift,
    small,
    small_land1,
    small_land2,
    scales,
    normed,
    outs,
    outs_land,
    load_sem,
    weight_sem,
    send_sem,
    recv_sem,
):
    row = lax.axis_index("row")
    head = lax.axis_index("head")
    x, z = row // SIDE, lax.rem(row, SIDE)
    rows = SIDE * SIDE
    blk = held.shape[0] // rows

    barrier = pltpu.get_barrier_semaphore()
    peers = []
    for d in (1, 2, 3):
        peers.append({"row": lax.rem(x + d, SIDE) * SIDE + z})
        peers.append({"row": x * SIDE + lax.rem(z + d, SIDE)})
    for d in range(1, HEADS):
        peers.append({"head": lax.rem(head + d, HEADS)})
    for peer in peers:
        pl.semaphore_signal(barrier, inc=1, device_id=peer, device_id_type=pl.DeviceIdType.MESH)

    def row_at(o, first, second):
        return first * SIDE + second if o == 0 else second * SIDE + first

    rings1 = [
        Ring(x, lambda a: row_at(0, a, z)),
        Ring(z, lambda a: row_at(1, a, x)),
    ]
    rings2 = [
        Ring(z, lambda b: row_at(0, x, b)),
        Ring(x, lambda b: row_at(1, z, b)),
    ]
    order = [[r.far, r.right, r.left, r.me] for r in rings1]

    load_hid = pltpu.make_async_copy(hid_hbm, hid, weight_sem.at[0])
    load_hid.start()
    loads = {}
    for j in range(SIDE):
        for o in (0, 1):
            for b in range(SIDE):
                n = (j * 2 + o) * SIDE + b
                at = row_at(o, order[o][j], b) * blk
                loads[j, o, b] = pltpu.make_async_copy(
                    state.at[pl.ds(at, blk), pl.ds(2 * o, 2)],
                    held.at[pl.ds(at, blk), pl.ds(2 * o, 2)],
                    load_sem.at[n],
                )
                loads[j, o, b].start()
    load_weights = []
    for n, (src, dst) in enumerate(((wv_hbm, wv), (wz_hbm, wz), (w_out_hbm, w_out))):
        load_weights.append(pltpu.make_async_copy(src, dst, weight_sem.at[n + 1]))
        load_weights[-1].start()

    w = jnp.concatenate(
        [
            wq[0].astype(F32),
            wq[1].astype(F32),
            wk[0].astype(F32),
            wk[1].astype(F32),
            wd[...].astype(F32),
            wb[...].astype(F32),
        ],
        axis=0,
    ).astype(BF16)
    col = lax.broadcasted_iota(jnp.int32, (COLS, 512), 0)
    lane = lax.broadcasted_iota(jnp.int32, (COLS, 512), 1)
    for hk in (0, 1):
        base = jnp.where(lane < 256, 16, 0) + 8 * hk
        spread[hk] = (col == base + lane % 8).astype(F32).astype(BF16)
    load_hid.wait()
    proj[...] = lax.dot_general(hid[...], w, NT, preferred_element_type=F32)

    q, k = proj[:, 0:16], proj[:, 16:32]
    sums = 0.0
    for n, product in enumerate((q * q, k * k, q * k)):
        seg = (
            lax.broadcasted_iota(jnp.int32, (8, 16), 1) // 8 + 2 * n == lax.broadcasted_iota(jnp.int32, (8, 16), 0)
        ).astype(F32)
        sums = sums + lax.dot_general(
            seg, product, NT, precision=lax.Precision.HIGHEST, preferred_element_type=F32
        )
    for a in range(SIDE):
        small[a] = sums[:, a * 128 : (a + 1) * 128]

    copies = Copies(send_sem, recv_sem)
    own_lane = lax.broadcasted_iota(jnp.int32, (4 * blk, 8 * blk), 1) // 8
    own_row = lax.rem(lax.broadcasted_iota(jnp.int32, (4 * blk, 8 * blk), 0), blk)
    own = own_lane == own_row

    def read_block(o, first, second):
        at = pl.multiple_of(row_at(o, first, second) * blk, blk)
        vec = jnp.concatenate(split(proj[pl.ds(at, blk), :]), axis=0)
        wide = jnp.dot(vec, spread[o], preferred_element_type=F32)
        wide = jnp.concatenate(
            [wide[:blk, : 8 * blk], wide[:blk, 8 * blk :], wide[blk:, : 8 * blk], wide[blk:, 8 * blk :]], axis=0
        )
        wide = jnp.where(own, wide, 0.0).astype(BF16)
        hi, lo = split(
            jnp.concatenate([held[pl.ds(at, blk), 2 * o + c].reshape(8 * blk, 128) for c in (0, 1)], axis=1)
        )
        main = jnp.dot(wide, hi, preferred_element_type=F32)
        rest = jnp.dot(wide[: 2 * blk], lo, preferred_element_type=F32)
        read = main[: 2 * blk] + (main[2 * blk :] + rest)
        for c in (0, 1):
            for t in (0, 1):
                part[o, c, t, first, second] = read[t * blk : (t + 1) * blk, c * 128 : (c + 1) * 128]

    def scatter1(o, t):
        return Scatter(copies, rings1[o], lambda c, a: part.at[o, c, t, a], land1.at[o, t])

    def own_piece(o, c, t):
        return part.at[o, c, t, rings1[o].me, rings2[o].me]

    def send2(o, t):
        s = Direct(copies, rings2[o])
        s.send(lambda b: part.at[o, :, t, rings1[o].me, b], lambda d: land2.at[o, t, d])
        return s

    def finish2(o, t, s):
        s.wait()
        for c in (0, 1):
            piece = own_piece(o, c, t)
            piece[...] = piece[...] + land2[o, t, 0, c] + land2[o, t, 1, c] + land2[o, t, 2, c]

    k1 = [scatter1(o, 0) for o in (0, 1)]
    q1 = [scatter1(o, 1) for o in (0, 1)]

    for j in range(SIDE):
        for o in (0, 1):
            for b in range(SIDE):
                loads[j, o, b].wait()
                read_block(o, order[o][j], b)
            if j == 0 and o == 0:
                pl.semaphore_wait(barrier, len(peers))
            if j == 0:
                k1[o].send_far()
            if j == 2:
                k1[o].send_near()
        if j == 0:
            small1 = Direct(copies, rings1[0])
            small1.send(lambda a: small.at[a], lambda d: small_land1.at[d])

    for s in q1:
        s.send_far()
    small1.wait()
    small[x] = small[x] + small_land1[0] + small_land1[1] + small_land1[2]
    small2 = Direct(copies, rings2[0])
    small2.send(lambda b: small.at[x], lambda d: small_land2.at[d])
    for s in k1:
        s.forward()
    for s in q1:
        s.send_near()

    mine = pl.ds(pl.multiple_of(row * blk, blk), blk)
    own_hid = hid[mine, :]
    chunks = own_hid.shape[1] // 256
    tall = jnp.concatenate([own_hid[:, n * 256 : (n + 1) * 256] for n in range(chunks)], axis=0)
    repeat = (
        lax.broadcasted_iota(jnp.int32, (256, 1024), 1) // 4 == lax.broadcasted_iota(jnp.int32, (256, 1024), 0)
    ).astype(F32).astype(BF16)
    tall = jnp.dot(tall, repeat, preferred_element_type=F32)
    at_head = lax.broadcasted_iota(jnp.int32, (blk, 1024), 1) % 4
    load_weights[0].wait()
    load_weights[1].wait()
    both = jnp.zeros((4 * blk, 256), F32)
    for n in range(chunks):
        piece = tall[n * blk : (n + 1) * blk]
        piece = jnp.concatenate([jnp.where(at_head == h, piece, 0.0).astype(BF16) for h in range(4)], axis=0)
        at = slice(n * 1024, (n + 1) * 1024)
        weights = jnp.concatenate([wv[at, :], wz[at, :]], axis=1)
        both = both + jnp.dot(piece, weights, preferred_element_type=F32)

    for s in q1:
        s.forward()
    for s in k1:
        s.finish()
    k2 = [send2(o, 0) for o in (0, 1)]

    decay_all[...] = jnp.exp(-jnp.exp(decay_log[...]) * softplus(proj[:, 32:36] + dt_bias[...]))
    own_t = lax.broadcasted_iota(jnp.int32, (8 * blk, 3 * blk), 0) // 8 == lax.rem(
        lax.broadcasted_iota(jnp.int32, (8 * blk, 3 * blk), 1), blk
    )
    picks = [
        (
            lax.broadcasted_iota(jnp.int32, (8 * blk, COLS), 1)
            == 16 + 8 * o + lax.broadcasted_iota(jnp.int32, (8 * blk, COLS), 0) % 8
        )
        .astype(F32)
        .astype(BF16)
        for o in (0, 1)
    ]

    def prepare(r, carry):
        at = pl.ds(pl.multiple_of(r * blk, blk), blk)
        hi, lo = split(proj[at, :])
        three = jnp.concatenate([hi.astype(F32), hi.astype(F32), lo.astype(F32)], axis=0).astype(BF16)
        decay = decay_all[at, :]
        for o in (0, 1):
            wide = lax.dot_general(picks[o], three, NT, preferred_element_type=F32)
            lift[r, o] = jnp.where(own_t, wide, 0.0).astype(BF16)
            for c in (0, 1):
                h = 2 * o + c
                keep = jnp.broadcast_to(decay[:, h : h + 1], (blk, 128))
                held[at, h] = keep[:, None, :] * held[at, h]
        return carry

    lax.fori_loop(0, rows // 2, prepare, 0)

    for s in q1:
        s.finish()
    q2 = [send2(o, 1) for o in (0, 1)]

    small2.wait()
    total = small[x] + small_land2[0] + small_land2[1] + small_land2[2]
    scales[...] = jnp.concatenate([total, jnp.zeros((120, 128), F32)], axis=0).T
    raw = scales[pl.ds(pl.multiple_of(z * blk, blk), blk), :]
    q_scale = lax.rsqrt(1.0 + raw[:, 0:2])
    k_scale = lax.rsqrt(1.0 + raw[:, 2:4])
    unit_dot = raw[:, 4:6] * q_scale * k_scale
    decay = decay_all[mine, :]
    beta = 1.0 / (1.0 + jnp.exp(-proj[mine, 36:40]))

    g1 = [
        Gather(
            copies,
            rings1[o],
            lambda c, a, o=o: delta_all.at[o, c, a],
            lambda a, o=o: delta_all.at[o, :, a],
        )
        for o in (0, 1)
    ]
    g2 = []
    deltas = []
    for o in (0, 1):
        finish2(o, 0, k2[o])
        for c in (0, 1):
            h = 2 * o + c
            readk = own_piece(o, c, 0)[...] * k_scale[:, o : o + 1]
            value = both[h * blk : (h + 1) * blk, :128]
            delta = beta[:, h : h + 1] * (value - decay[:, h : h + 1] * readk)
            delta_all[o, c, rings1[o].me, rings2[o].me] = delta * k_scale[:, o : o + 1]
            deltas.append(delta)
        g2.append(Direct(copies, rings2[o]))
        here = delta_all.at[o, :, rings1[o].me, rings2[o].me]
        g2[o].send(lambda b: here, lambda d: here)

    lax.fori_loop(rows // 2, rows, prepare, 0)

    for o in (0, 1):
        finish2(o, 1, q2[o])
        for c in (0, 1):
            h = 2 * o + c
            old = own_piece(o, c, 1)[...] * q_scale[:, o : o + 1]
            readq = decay[:, h : h + 1] * old + unit_dot[:, o : o + 1] * deltas[h]
            meansq = jnp.mean(readq * readq, axis=-1, keepdims=True)
            gate = both[h * blk : (h + 1) * blk, 128:]
            gate = gate / (1.0 + jnp.exp(-gate))
            normed[:, h * 128 : (h + 1) * 128] = (readq * lax.rsqrt(meansq + 0.5) * gain[...] * gate).astype(BF16)

    load_weights[2].wait()
    width = outs.shape[-1]
    for n in range(HEADS):
        outs[n] = jnp.dot(normed[...], w_out[:, n * width : (n + 1) * width], preferred_element_type=F32)
    out_copies = []
    for d in range(1, HEADS):
        to = lax.rem(head + d, HEADS)
        out_copies.append(copies.start(outs.at[to], outs_land.at[head], {"head": to}))
    outs_land[head] = outs[head]

    for o in (0, 1):
        g2[o].wait()
        g1[o].send()

    def update(o, first, second):
        r = row_at(o, first, second)
        at = pl.ds(pl.multiple_of(r * blk, blk), blk)
        hi, lo = split(jnp.concatenate([delta_all[o, c, first, second] for c in (0, 1)], axis=1))
        add = jnp.dot(lift[r, o], jnp.concatenate([hi, lo, hi], axis=0), preferred_element_type=F32)
        for c in (0, 1):
            h = 2 * o + c
            held[at, h] = held[at, h] + add[:, c * 128 : (c + 1) * 128].reshape(blk, 8, 128)

    def update_rows(o, first):
        def body(b, carry):
            update(o, first, b)
            return carry

        lax.fori_loop(0, SIDE, body, 0)

    for o in (0, 1):
        update_rows(o, rings1[o].me)
    for o in (0, 1):
        g1[o].forward()
    for o in (0, 1):
        update_rows(o, rings1[o].left)
        update_rows(o, rings1[o].right)
    for copy in out_copies:
        copy.wait_recv()
    total_out = outs_land[0]
    for n in range(1, HEADS):
        total_out = total_out + outs_land[n]
    layer_out[...] = total_out.astype(BF16)
    for o in (0, 1):
        g1[o].finish()
        update_rows(o, rings1[o].far)
    for copy in copies.made:
        copy.wait_send()


def local(
    hidden_in,
    w_query,
    w_key,
    w_value,
    w_zgate,
    w_decay,
    w_beta,
    decay_log,
    dt_bias,
    norm_gain,
    w_out,
    state,
):
    seqs, width = hidden_in.shape
    rows = SIDE * SIDE
    blk = seqs // rows
    vmem = pl.BlockSpec(memory_space=pltpu.VMEM)
    anywhere = pl.BlockSpec(memory_space=pltpu.HBM)
    n_copies = 2 * 3 + 4 * 6 + 4 * 3 + 2 * 3 + 2 * 4 + HEADS - 1
    return pl.pallas_call(
        exchange_kernel,
        out_shape=(
            jax.ShapeDtypeStruct((blk, 256), BF16),
            pltpu.VMEM(state.shape, F32),
        ),
        in_specs=[vmem] * 7 + [anywhere] * 5,
        out_specs=(vmem, vmem),
        scratch_shapes=[
            pltpu.VMEM((seqs, width), BF16),
            pltpu.VMEM((4 * width, 128), BF16),
            pltpu.VMEM((4 * width, 128), BF16),
            pltpu.VMEM((512, width), BF16),
            pltpu.VMEM((seqs, COLS), F32),
            pltpu.VMEM((seqs, 4), F32),
            pltpu.VMEM((2, COLS, 512), BF16),
            pltpu.VMEM((2, 2, 2, SIDE, SIDE, blk, 128), F32),
            pltpu.VMEM((2, 2, 2, 3, SIDE, blk, 128), F32),
            pltpu.VMEM((2, 2, 3, 2, blk, 128), F32),
            pltpu.VMEM((2, 2, SIDE, SIDE, blk, 128), F32),
            pltpu.VMEM((rows, 2, 8 * blk, 3 * blk), BF16),
            pltpu.VMEM((SIDE, 8, 128), F32),
            pltpu.VMEM((3, 8, 128), F32),
            pltpu.VMEM((3, 8, 128), F32),
            pltpu.VMEM((128, 128), F32),
            pltpu.VMEM((blk, 512), BF16),
            pltpu.VMEM((HEADS, blk, 256), F32),
            pltpu.VMEM((HEADS, blk, 256), F32),
            pltpu.SemaphoreType.DMA((32,)),
            pltpu.SemaphoreType.DMA((4,)),
            pltpu.SemaphoreType.DMA((n_copies,)),
            pltpu.SemaphoreType.DMA((n_copies,)),
        ],
        compiler_params=pltpu.CompilerParams(
            collective_id=0, has_side_effects=True, vmem_limit_bytes=36 * 1024 * 1024
        ),
        name="exchange",
    )(
        *(
            pltpu.with_memory_space_constraint(operand, pltpu.HBM)
            for operand in (
                jnp.transpose(w_query, (1, 2, 0)),
                jnp.transpose(w_key, (1, 2, 0)),
                jnp.transpose(w_decay, (1, 0)),
                jnp.transpose(w_beta, (1, 0)),
                decay_log.reshape(1, 4),
                dt_bias.reshape(1, 4),
                norm_gain.reshape(1, 128),
                hidden_in,
                w_value.reshape(4 * width, 128),
                w_zgate.reshape(4 * width, 128),
                w_out.reshape(512, width),
                state,
            )
        )
    )


def solution(mesh):
    in_specs = (
        P(),
        P(None, "head", "row"),
        P(None, "head", "row"),
        P(None, "head", None),
        P(None, "head", None),
        P(None, "head"),
        P(None, "head"),
        P("head"),
        P("head"),
        P(),
        P("head", None, None),
        P(None, "head", "row", None),
    )
    out_specs = (P("row", "head"), P(None, "head", "row", None))
    return jax.shard_map(local, mesh=mesh, in_specs=in_specs, out_specs=out_specs, check_vma=False)
```

time: 69.2 us -> 50.6 us (0.73)
  Pallas kernels: 60.4 us -> 45.8 us
  matrix products: 3.58 us -> 0 us
    pallas_call x2 -> x1, Pallas kernels: 60.4 us -> 45.8 us  [local(): pl.pallas_call(exchange_kernel, out_shape=(jax.ShapeDtypeStruct((blk, 256...]
    dot_general x2 -> x0, matrix products: 3.58 us -> none  [the longest x1 2.06 us: local(): jnp.einsum('bd,dhv->bhv', own_hidden, w_zgate, preferred_element_type=F32)]
    unnamed x25 -> x2, local copies, waits for them, and re-layouts: 3.9 us -> 4 us
where the time goes in v2:
time: 50.6 us; the launch traced here: 50.5 us
  Pallas kernels  45.8 us (91%)
  local copies, waits for them, and re-layouts  4 us (8%)
  between operations  0.64 us (1%)
    pallas_call x1, Pallas kernels, local(): pl.pallas_call(exchange_kernel, out_shape=(jax.ShapeDtypeStruct((blk, 256...  45.8 us
    unnamed x2, local copies, waits for them, and re-layouts  4 us

profile of v2, /device:TPU:0, one launch (start us, length us, event | category | flops | bytes accessed | tf_op | source)
XLA Modules:
  0.0 50.5 jit_solution(16833542931825703830)
XLA Ops:
  0.6 45.8 %exchange.1 = (bf16[32,256]{1,0:T(8,128)(2,1)S(1)}, f32[512,4,8,128]{3,2,1,0:T(8,128)S(1)}) custom-call(bf16[2,8,2048]{2,1,0:T(8,128)(2,1)} %bitcast.13, bf16[2,8,2048]{2,1,0:T(8,128)(2,1)} %bitcast.14, bf16[4,2048]{1,0:T(4,128)(2,1)} %bitcast.15, bf16[4,2048]{1,0:T(4,128)(2,1)} %bitcast.16, f32[1,4]{1,0:T(1,128)} %bitcast.17, f32[1,4]{1,0:T(1,128)} %bitcast.18, ...), custom_call_target="tpu_custom_call" | custom-call | tf_op jit(solution)/shard_map/exchange/pallas_call | solution.py:494
  46.5 3.4 %copy.16 = f32[512,4,8,128]{3,2,1,0:T(8,128)} copy(f32[512,4,8,128]{3,2,1,0:T(8,128)S(1)} %get-tuple-element.3) | data formatting | bytes 16777216
  49.9 0.6 %copy.17 = bf16[32,256]{1,0:T(8,128)(2,1)} copy(bf16[32,256]{1,0:T(8,128)(2,1)S(1)} %get-tuple-element.6) | data formatting | bytes 32768

commit v3 on v2

--- a/solution.py
+++ b/solution.py
@@ -90,7 +90,7 @@
 
     def send(self, src, dst):
         r = self.ring
-        for d, (at, peer) in enumerate(((r.right, r.to_right), (r.left, r.to_left), (r.far, r.to_far))):
+        for d, (at, peer) in enumerate(((r.far, r.to_far), (r.right, r.to_right), (r.left, r.to_left))):
             self.sent.append(self.copies.start(src(at), dst(d), peer))
 
     def wait(self):
@@ -129,10 +129,10 @@
 
 
 def exchange_kernel(
-    wq,
-    wk,
-    wd,
-    wb,
+    wq_hbm,
+    wk_hbm,
+    wd_hbm,
+    wb_hbm,
     decay_log,
     dt_bias,
     gain,
@@ -143,6 +143,10 @@
     state,
     layer_out,
     held,
+    wq,
+    wk,
+    wd,
+    wb,
     hid,
     wv,
     wz,
@@ -196,8 +200,13 @@
     ]
     order = [[r.far, r.right, r.left, r.me] for r in rings1]
 
-    load_hid = pltpu.make_async_copy(hid_hbm, hid, weight_sem.at[0])
-    load_hid.start()
+    first = []
+    small_weights = ((wq_hbm, wq), (wk_hbm, wk), (wd_hbm, wd), (wb_hbm, wb))
+    quarter = hid.shape[0] // 4
+    pieces = tuple((hid_hbm.at[pl.ds(n * quarter, quarter)], hid.at[pl.ds(n * quarter, quarter)]) for n in range(4))
+    for n, (src, dst) in enumerate(small_weights + pieces):
+        first.append(pltpu.make_async_copy(src, dst, weight_sem.at[n]))
+        first[-1].start()
     loads = {}
     for j in range(SIDE):
         for o in (0, 1):
@@ -209,12 +218,20 @@
                     held.at[pl.ds(at, blk), pl.ds(2 * o, 2)],
                     load_sem.at[n],
                 )
+                if j == 0:
+                    loads[j, o, b].start()
+
+    col = lax.broadcasted_iota(jnp.int32, (COLS, 512), 0)
+    lane = lax.broadcasted_iota(jnp.int32, (COLS, 512), 1)
+    for hk in (0, 1):
+        base = jnp.where(lane < 256, 16, 0) + 8 * hk
+        spread[hk] = (col == base + lane % 8).astype(F32).astype(BF16)
+    for copy in first:
+        copy.wait()
+    for j in (1, 2, 3):
+        for o in (0, 1):
+            for b in range(SIDE):
                 loads[j, o, b].start()
-    load_weights = []
-    for n, (src, dst) in enumerate(((wv_hbm, wv), (wz_hbm, wz), (w_out_hbm, w_out))):
-        load_weights.append(pltpu.make_async_copy(src, dst, weight_sem.at[n + 1]))
-        load_weights[-1].start()
-
     w = jnp.concatenate(
         [
             wq[0].astype(F32),
@@ -226,25 +243,7 @@
         ],
         axis=0,
     ).astype(BF16)
-    col = lax.broadcasted_iota(jnp.int32, (COLS, 512), 0)
-    lane = lax.broadcasted_iota(jnp.int32, (COLS, 512), 1)
-    for hk in (0, 1):
-        base = jnp.where(lane < 256, 16, 0) + 8 * hk
-        spread[hk] = (col == base + lane % 8).astype(F32).astype(BF16)
-    load_hid.wait()
     proj[...] = lax.dot_general(hid[...], w, NT, preferred_element_type=F32)
-
-    q, k = proj[:, 0:16], proj[:, 16:32]
-    sums = 0.0
-    for n, product in enumerate((q * q, k * k, q * k)):
-        seg = (
-            lax.broadcasted_iota(jnp.int32, (8, 16), 1) // 8 + 2 * n == lax.broadcasted_iota(jnp.int32, (8, 16), 0)
-        ).astype(F32)
-        sums = sums + lax.dot_general(
-            seg, product, NT, precision=lax.Precision.HIGHEST, preferred_element_type=F32
-        )
-    for a in range(SIDE):
-        small[a] = sums[:, a * 128 : (a + 1) * 128]
 
     copies = Copies(send_sem, recv_sem)
     own_lane = lax.broadcasted_iota(jnp.int32, (4 * blk, 8 * blk), 1) // 8
@@ -293,23 +292,40 @@
         for o in (0, 1):
             for b in range(SIDE):
                 loads[j, o, b].wait()
-                read_block(o, order[o][j], b)
-            if j == 0 and o == 0:
-                pl.semaphore_wait(barrier, len(peers))
             if j == 0:
+                for b in range(SIDE):
+                    read_block(o, order[o][j], b)
+                if o == 0:
+                    pl.semaphore_wait(barrier, len(peers))
                 k1[o].send_far()
-            if j == 2:
+        if j > 0:
+            for o in (0, 1):
+                for b in range(SIDE):
+                    read_block(o, order[o][j], b)
+        if j == 2:
+            for o in (0, 1):
                 k1[o].send_near()
-        if j == 0:
-            small1 = Direct(copies, rings1[0])
-            small1.send(lambda a: small.at[a], lambda d: small_land1.at[d])
-
     for s in q1:
         s.send_far()
-    small1.wait()
-    small[x] = small[x] + small_land1[0] + small_land1[1] + small_land1[2]
-    small2 = Direct(copies, rings2[0])
-    small2.send(lambda b: small.at[x], lambda d: small_land2.at[d])
+    load_weights = []
+    for n, (src, dst) in enumerate(((wv_hbm, wv), (wz_hbm, wz), (w_out_hbm, w_out))):
+        load_weights.append(pltpu.make_async_copy(src, dst, weight_sem.at[n + 8]))
+        load_weights[-1].start()
+
+    q, k = proj[:, 0:16], proj[:, 16:32]
+    sums = 0.0
+    for n, product in enumerate((q * q, k * k, q * k)):
+        seg = (
+            lax.broadcasted_iota(jnp.int32, (8, 16), 1) // 8 + 2 * n == lax.broadcasted_iota(jnp.int32, (8, 16), 0)
+        ).astype(F32)
+        sums = sums + lax.dot_general(
+            seg, product, NT, precision=lax.Precision.HIGHEST, preferred_element_type=F32
+        )
+    for a in range(SIDE):
+        small[a] = sums[:, a * 128 : (a + 1) * 128]
+
+    small1 = Direct(copies, rings1[0])
+    small1.send(lambda a: small.at[a], lambda d: small_land1.at[d])
     for s in k1:
         s.forward()
     for s in q1:
@@ -334,6 +350,10 @@
         weights = jnp.concatenate([wv[at, :], wz[at, :]], axis=1)
         both = both + jnp.dot(piece, weights, preferred_element_type=F32)
 
+    small1.wait()
+    small[x] = small[x] + small_land1[0] + small_land1[1] + small_land1[2]
+    small2 = Direct(copies, rings2[0])
+    small2.send(lambda b: small.at[x], lambda d: small_land2.at[d])
     for s in q1:
         s.forward()
     for s in k1:
@@ -384,15 +404,19 @@
     decay = decay_all[mine, :]
     beta = 1.0 / (1.0 + jnp.exp(-proj[mine, 36:40]))
 
-    g1 = [
-        Gather(
+    def gather1(o, b):
+        return Gather(
             copies,
             rings1[o],
-            lambda c, a, o=o: delta_all.at[o, c, a],
-            lambda a, o=o: delta_all.at[o, :, a],
+            lambda c, a: delta_all.at[o, c, a, b],
+            lambda a: delta_all.at[o, :, a, b],
         )
-        for o in (0, 1)
-    ]
+
+    g1 = {}
+    for o in (0, 1):
+        r = rings2[o]
+        for name, b in (("me", r.me), ("far", r.far), ("left", r.left), ("right", r.right)):
+            g1[o, name] = gather1(o, b)
     g2 = []
     deltas = []
     for o in (0, 1):
@@ -407,8 +431,17 @@
         g2.append(Direct(copies, rings2[o]))
         here = delta_all.at[o, :, rings1[o].me, rings2[o].me]
         g2[o].send(lambda b: here, lambda d: here)
+        g1[o, "me"].send()
 
     lax.fori_loop(rows // 2, rows, prepare, 0)
+    for o in (0, 1):
+        for n, name in ((1, "left"), (2, "right")):
+            g2[o].sent[n].wait_recv()
+            g1[o, name].send()
+    for o in (0, 1):
+        g1[o, "me"].forward()
+        g2[o].sent[0].wait_recv()
+        g1[o, "far"].send()
 
     for o in (0, 1):
         finish2(o, 1, q2[o])
@@ -432,8 +465,8 @@
     outs_land[head] = outs[head]
 
     for o in (0, 1):
-        g2[o].wait()
-        g1[o].send()
+        for name in ("left", "right"):
+            g1[o, name].forward()
 
     def update(o, first, second):
         r = row_at(o, first, second)
@@ -445,16 +478,13 @@
             held[at, h] = held[at, h] + add[:, c * 128 : (c + 1) * 128].reshape(blk, 8, 128)
 
     def update_rows(o, first):
-        def body(b, carry):
+        for b in range(SIDE):
             update(o, first, b)
-            return carry
-
-        lax.fori_loop(0, SIDE, body, 0)
 
     for o in (0, 1):
         update_rows(o, rings1[o].me)
     for o in (0, 1):
-        g1[o].forward()
+        g1[o, "far"].forward()
     for o in (0, 1):
         update_rows(o, rings1[o].left)
         update_rows(o, rings1[o].right)
@@ -464,8 +494,9 @@
     for n in range(1, HEADS):
         total_out = total_out + outs_land[n]
     layer_out[...] = total_out.astype(BF16)
-    for o in (0, 1):
-        g1[o].finish()
+    for g in g1.values():
+        g.finish()
+    for o in (0, 1):
         update_rows(o, rings1[o].far)
     for copy in copies.made:
         copy.wait_send()
@@ -490,16 +521,20 @@
     blk = seqs // rows
     vmem = pl.BlockSpec(memory_space=pltpu.VMEM)
     anywhere = pl.BlockSpec(memory_space=pltpu.HBM)
-    n_copies = 2 * 3 + 4 * 6 + 4 * 3 + 2 * 3 + 2 * 4 + HEADS - 1
+    n_copies = 2 * 3 + 4 * 6 + 4 * 3 + 2 * 3 + 2 * 4 * 4 + HEADS - 1
     return pl.pallas_call(
         exchange_kernel,
         out_shape=(
             jax.ShapeDtypeStruct((blk, 256), BF16),
             pltpu.VMEM(state.shape, F32),
         ),
-        in_specs=[vmem] * 7 + [anywhere] * 5,
+        in_specs=[anywhere] * 4 + [vmem] * 3 + [anywhere] * 5,
         out_specs=(vmem, vmem),
         scratch_shapes=[
+            pltpu.VMEM((2, 8, width), BF16),
+            pltpu.VMEM((2, 8, width), BF16),
+            pltpu.VMEM((4, width), BF16),
+            pltpu.VMEM((4, width), BF16),
             pltpu.VMEM((seqs, width), BF16),
             pltpu.VMEM((4 * width, 128), BF16),
             pltpu.VMEM((4 * width, 128), BF16),
@@ -520,7 +555,7 @@
             pltpu.VMEM((HEADS, blk, 256), F32),
             pltpu.VMEM((HEADS, blk, 256), F32),
             pltpu.SemaphoreType.DMA((32,)),
-            pltpu.SemaphoreType.DMA((4,)),
+            pltpu.SemaphoreType.DMA((11,)),
             pltpu.SemaphoreType.DMA((n_copies,)),
             pltpu.SemaphoreType.DMA((n_copies,)),
         ],

time: 50.6 us -> 42.4 us (0.84)
  Pallas kernels: 45.8 us -> 37.7 us
    pallas_call x1, Pallas kernels: 45.8 us -> 37.7 us  [local(): pl.pallas_call(exchange_kernel, out_shape=(jax.ShapeDtypeStruct((blk, 256...]
where the time goes in v3:
time: 42.4 us; the launch traced here: 42.3 us
  Pallas kernels  37.7 us (89%)
  local copies, waits for them, and re-layouts  4 us (9%)
  between operations  0.64 us (2%)
    pallas_call x1, Pallas kernels, local(): pl.pallas_call(exchange_kernel, out_shape=(jax.ShapeDtypeStruct((blk, 256...  37.7 us
    unnamed x2, local copies, waits for them, and re-layouts  4 us

profile of v3, /device:TPU:0, one launch (start us, length us, event | category | flops | bytes accessed | tf_op | source)
XLA Modules:
  0.0 42.3 jit_solution(6045187429562523621)
XLA Ops:
  0.6 37.7 %exchange.1 = (bf16[32,256]{1,0:T(8,128)(2,1)S(1)}, f32[512,4,8,128]{3,2,1,0:T(8,128)S(1)}) custom-call(bf16[2,8,2048]{2,1,0:T(8,128)(2,1)} %bitcast.13, bf16[2,8,2048]{2,1,0:T(8,128)(2,1)} %bitcast.14, bf16[4,2048]{1,0:T(4,128)(2,1)} %bitcast.15, bf16[4,2048]{1,0:T(4,128)(2,1)} %bitcast.16, f32[1,4]{1,0:T(1,128)} %bitcast.17, f32[1,4]{1,0:T(1,128)} %bitcast.18, ...), custom_call_target="tpu_custom_call" | custom-call | tf_op jit(solution)/shard_map/exchange/pallas_call | solution.py:525
  38.3 3.4 %copy.16 = f32[512,4,8,128]{3,2,1,0:T(8,128)} copy(f32[512,4,8,128]{3,2,1,0:T(8,128)S(1)} %get-tuple-element.3) | data formatting | bytes 16777216
  41.7 0.6 %copy.17 = bf16[32,256]{1,0:T(8,128)(2,1)} copy(bf16[32,256]{1,0:T(8,128)(2,1)S(1)} %get-tuple-element.6) | data formatting | bytes 32768

commit v4 on v3

--- a/solution.py
+++ b/solution.py
@@ -60,12 +60,13 @@
             self.copies.start(self.part(1, r.far), self.land.at[1, 0], r.to_right),
         ]
 
-    def send_near(self):
+    def send_right(self):
         r = self.ring
-        self.direct = [
-            self.copies.start(self.part(0, r.right), self.land.at[0, 1], r.to_right),
-            self.copies.start(self.part(1, r.left), self.land.at[1, 1], r.to_left),
-        ]
+        self.direct = [self.copies.start(self.part(0, r.right), self.land.at[0, 1], r.to_right)]
+
+    def send_left(self):
+        r = self.ring
+        self.direct.append(self.copies.start(self.part(1, r.left), self.land.at[1, 1], r.to_left))
 
     def forward(self):
         r = self.ring
@@ -126,6 +127,12 @@
 def split(x):
     hi = x.astype(BF16)
     return hi, (x - hi.astype(F32)).astype(BF16)
+
+
+def growth(delta_all, lift, o, first, second, r):
+    hi, lo = split(jnp.concatenate([delta_all[o, c, first, second] for c in (0, 1)], axis=1))
+    add = jnp.dot(lift[r, o], jnp.concatenate([hi, lo, hi], axis=0), preferred_element_type=F32)
+    return [add[:, c * 128 : (c + 1) * 128].reshape(hi.shape[0], 8, 128) for c in (0, 1)]
 
 
 def exchange_kernel(
@@ -141,8 +148,10 @@
     wz_hbm,
     w_out_hbm,
     state,
-    layer_out,
     held,
+    delta_all,
+    lift,
+    outs_land,
     wq,
     wk,
     wd,
@@ -157,15 +166,12 @@
     part,
     land1,
     land2,
-    delta_all,
-    lift,
     small,
     small_land1,
     small_land2,
     scales,
     normed,
     outs,
-    outs_land,
     load_sem,
     weight_sem,
     send_sem,
@@ -218,20 +224,17 @@
                     held.at[pl.ds(at, blk), pl.ds(2 * o, 2)],
                     load_sem.at[n],
                 )
-                if j == 0:
-                    loads[j, o, b].start()
 
     col = lax.broadcasted_iota(jnp.int32, (COLS, 512), 0)
     lane = lax.broadcasted_iota(jnp.int32, (COLS, 512), 1)
     for hk in (0, 1):
         base = jnp.where(lane < 256, 16, 0) + 8 * hk
         spread[hk] = (col == base + lane % 8).astype(F32).astype(BF16)
-    for copy in first:
+    for copy in first[:5]:
         copy.wait()
-    for j in (1, 2, 3):
-        for o in (0, 1):
-            for b in range(SIDE):
-                loads[j, o, b].start()
+    for o in (0, 1):
+        for b in range(SIDE):
+            loads[0, o, b].start()
     w = jnp.concatenate(
         [
             wq[0].astype(F32),
@@ -243,7 +246,19 @@
         ],
         axis=0,
     ).astype(BF16)
-    proj[...] = lax.dot_general(hid[...], w, NT, preferred_element_type=F32)
+    for n in range(4):
+        if n > 0:
+            first[4 + n].wait()
+        if n == 2:
+            for o in (0, 1):
+                for b in range(SIDE):
+                    loads[1, o, b].start()
+        at = pl.ds(n * quarter, quarter)
+        proj[at, :] = lax.dot_general(hid[at, :], w, NT, preferred_element_type=F32)
+    for j in (2, 3):
+        for o in (0, 1):
+            for b in range(SIDE):
+                loads[j, o, b].start()
 
     copies = Copies(send_sem, recv_sem)
     own_lane = lax.broadcasted_iota(jnp.int32, (4 * blk, 8 * blk), 1) // 8
@@ -298,15 +313,24 @@
                 if o == 0:
                     pl.semaphore_wait(barrier, len(peers))
                 k1[o].send_far()
-        if j > 0:
+        if j == 0:
+            for o in (0, 1):
+                q1[o].send_far()
+        else:
             for o in (0, 1):
                 for b in range(SIDE):
                     read_block(o, order[o][j], b)
+        if j == 1:
+            for o in (0, 1):
+                k1[o].send_right()
         if j == 2:
             for o in (0, 1):
-                k1[o].send_near()
+                k1[o].send_left()
+    for s in k1:
+        s.forward()
     for s in q1:
-        s.send_far()
+        s.send_right()
+        s.send_left()
     load_weights = []
     for n, (src, dst) in enumerate(((wv_hbm, wv), (wz_hbm, wz), (w_out_hbm, w_out))):
         load_weights.append(pltpu.make_async_copy(src, dst, weight_sem.at[n + 8]))
@@ -326,10 +350,8 @@
 
     small1 = Direct(copies, rings1[0])
     small1.send(lambda a: small.at[a], lambda d: small_land1.at[d])
-    for s in k1:
+    for s in q1:
         s.forward()
-    for s in q1:
-        s.send_near()
 
     mine = pl.ds(pl.multiple_of(row * blk, blk), blk)
     own_hid = hid[mine, :]
@@ -354,8 +376,6 @@
     small[x] = small[x] + small_land1[0] + small_land1[1] + small_land1[2]
     small2 = Direct(copies, rings2[0])
     small2.send(lambda b: small.at[x], lambda d: small_land2.at[d])
-    for s in q1:
-        s.forward()
     for s in k1:
         s.finish()
     k2 = [send2(o, 0) for o in (0, 1)]
@@ -435,15 +455,6 @@
 
     lax.fori_loop(rows // 2, rows, prepare, 0)
     for o in (0, 1):
-        for n, name in ((1, "left"), (2, "right")):
-            g2[o].sent[n].wait_recv()
-            g1[o, name].send()
-    for o in (0, 1):
-        g1[o, "me"].forward()
-        g2[o].sent[0].wait_recv()
-        g1[o, "far"].send()
-
-    for o in (0, 1):
         finish2(o, 1, q2[o])
         for c in (0, 1):
             h = 2 * o + c
@@ -465,21 +476,26 @@
     outs_land[head] = outs[head]
 
     for o in (0, 1):
+        for n, name in ((1, "left"), (2, "right")):
+            g2[o].sent[n].wait_recv()
+            g1[o, name].send()
+    for o in (0, 1):
+        g1[o, "me"].forward()
+        g2[o].sent[0].wait_recv()
+        g1[o, "far"].send()
+
+    for o in (0, 1):
         for name in ("left", "right"):
             g1[o, name].forward()
 
-    def update(o, first, second):
-        r = row_at(o, first, second)
-        at = pl.ds(pl.multiple_of(r * blk, blk), blk)
-        hi, lo = split(jnp.concatenate([delta_all[o, c, first, second] for c in (0, 1)], axis=1))
-        add = jnp.dot(lift[r, o], jnp.concatenate([hi, lo, hi], axis=0), preferred_element_type=F32)
-        for c in (0, 1):
-            h = 2 * o + c
-            held[at, h] = held[at, h] + add[:, c * 128 : (c + 1) * 128].reshape(blk, 8, 128)
-
     def update_rows(o, first):
         for b in range(SIDE):
-            update(o, first, b)
+            r = row_at(o, first, b)
+            at = pl.ds(pl.multiple_of(r * blk, blk), blk)
+            add = growth(delta_all, lift, o, first, b, r)
+            for c in (0, 1):
+                h = 2 * o + c
+                held[at, h] = held[at, h] + add[c]
 
     for o in (0, 1):
         update_rows(o, rings1[o].me)
@@ -490,16 +506,45 @@
         update_rows(o, rings1[o].right)
     for copy in out_copies:
         copy.wait_recv()
-    total_out = outs_land[0]
-    for n in range(1, HEADS):
-        total_out = total_out + outs_land[n]
-    layer_out[...] = total_out.astype(BF16)
     for g in g1.values():
         g.finish()
-    for o in (0, 1):
-        update_rows(o, rings1[o].far)
     for copy in copies.made:
         copy.wait_send()
+
+
+def finish_kernel(held, delta_all, lift, outs_land, layer_out, new_state, last, sems):
+    row = lax.axis_index("row")
+    spots = (row // SIDE, lax.rem(row, SIDE))
+    blk = held.shape[0] // (SIDE * SIDE)
+    made = []
+
+    def store(src, o, r, count=1):
+        dst = new_state.at[pl.ds(pl.multiple_of(r * blk, blk), count * blk), pl.ds(2 * o, 2)]
+        made.append(pltpu.make_async_copy(src, dst, sems.at[len(made)]))
+        made[-1].start()
+
+    for d in (0, 1, 3):
+        first = lax.rem(spots[0] + d, SIDE)
+        at = pl.ds(pl.multiple_of(first * SIDE * blk, blk), SIDE * blk)
+        store(held.at[at, pl.ds(0, 2)], 0, first * SIDE, SIDE)
+        for b in range(SIDE):
+            r = b * SIDE + lax.rem(spots[1] + d, SIDE)
+            store(held.at[pl.ds(pl.multiple_of(r * blk, blk), blk), pl.ds(2, 2)], 1, r)
+    for o in (0, 1):
+        first = lax.rem(spots[o] + 2, SIDE)
+        for b in range(SIDE):
+            r = first * SIDE + b if o == 0 else b * SIDE + first
+            at = pl.ds(pl.multiple_of(r * blk, blk), blk)
+            add = growth(delta_all, lift, o, first, b, r)
+            for c in (0, 1):
+                last[o * SIDE + b, :, c] = held[at, 2 * o + c] + add[c]
+            store(last.at[o * SIDE + b], o, r)
+    total = outs_land[0]
+    for n in range(1, HEADS):
+        total = total + outs_land[n]
+    layer_out[...] = total.astype(BF16)
+    for copy in made:
+        copy.wait()
 
 
 def local(
@@ -522,14 +567,16 @@
     vmem = pl.BlockSpec(memory_space=pltpu.VMEM)
     anywhere = pl.BlockSpec(memory_space=pltpu.HBM)
     n_copies = 2 * 3 + 4 * 6 + 4 * 3 + 2 * 3 + 2 * 4 * 4 + HEADS - 1
-    return pl.pallas_call(
+    held, delta_all, lift, outs_land = pl.pallas_call(
         exchange_kernel,
         out_shape=(
-            jax.ShapeDtypeStruct((blk, 256), BF16),
             pltpu.VMEM(state.shape, F32),
+            pltpu.VMEM((2, 2, SIDE, SIDE, blk, 128), F32),
+            pltpu.VMEM((rows, 2, 8 * blk, 3 * blk), BF16),
+            pltpu.VMEM((HEADS, blk, 256), F32),
         ),
         in_specs=[anywhere] * 4 + [vmem] * 3 + [anywhere] * 5,
-        out_specs=(vmem, vmem),
+        out_specs=(vmem,) * 4,
         scratch_shapes=[
             pltpu.VMEM((2, 8, width), BF16),
             pltpu.VMEM((2, 8, width), BF16),
@@ -545,14 +592,11 @@
             pltpu.VMEM((2, 2, 2, SIDE, SIDE, blk, 128), F32),
             pltpu.VMEM((2, 2, 2, 3, SIDE, blk, 128), F32),
             pltpu.VMEM((2, 2, 3, 2, blk, 128), F32),
-            pltpu.VMEM((2, 2, SIDE, SIDE, blk, 128), F32),
-            pltpu.VMEM((rows, 2, 8 * blk, 3 * blk), BF16),
             pltpu.VMEM((SIDE, 8, 128), F32),
             pltpu.VMEM((3, 8, 128), F32),
             pltpu.VMEM((3, 8, 128), F32),
             pltpu.VMEM((128, 128), F32),
             pltpu.VMEM((blk, 512), BF16),
-            pltpu.VMEM((HEADS, blk, 256), F32),
             pltpu.VMEM((HEADS, blk, 256), F32),
             pltpu.SemaphoreType.DMA((32,)),
             pltpu.SemaphoreType.DMA((11,)),
@@ -582,6 +626,22 @@
             )
         )
     )
+    layer_out, new_state = pl.pallas_call(
+        finish_kernel,
+        out_shape=(
+            jax.ShapeDtypeStruct((blk, 256), BF16),
+            jax.ShapeDtypeStruct(state.shape, F32),
+        ),
+        in_specs=[vmem] * 4,
+        out_specs=(vmem, anywhere),
+        scratch_shapes=[
+            pltpu.VMEM((2 * SIDE, blk, 2, 8, 128), F32),
+            pltpu.SemaphoreType.DMA((23,)),
+        ],
+        compiler_params=pltpu.CompilerParams(vmem_limit_bytes=16 * 1024 * 1024),
+        name="finish",
+    )(*(pltpu.with_memory_space_constraint(a, pltpu.VMEM) for a in (held, delta_all, lift, outs_land)))
+    return layer_out, new_state
 
 
 def solution(mesh):

time: 42.4 us -> 41.7 us (0.983)
  local copies, waits for them, and re-layouts: 4 us -> 0 us
  Pallas kernels: 37.7 us -> 41 us
    unnamed x2 -> x0, local copies, waits for them, and re-layouts: 4 us -> none
    pallas_call x1 -> x2, Pallas kernels: 37.7 us -> 41 us  [the longest x1 36.9 us: local(): pl.pallas_call(exchange_kernel, out_shape=(pltpu.VMEM(state.shape, F32),...]
where the time goes in v4:
time: 41.7 us; the launch traced here: 41.6 us
  Pallas kernels  41 us (98%)
  between operations  0.64 us (2%)
    pallas_call x1, Pallas kernels, local(): pl.pallas_call(exchange_kernel, out_shape=(pltpu.VMEM(state.shape, F32),...  36.9 us
    pallas_call x1, Pallas kernels, local(): pl.pallas_call(finish_kernel, out_shape=(jax.ShapeDtypeStruct((blk, 256),...  4.1 us

profile of v4, /device:TPU:0, one launch (start us, length us, event | category | flops | bytes accessed | tf_op | source)
XLA Modules:
  0.0 41.6 jit_solution(17690522275269450111)
XLA Ops:
  0.6 36.9 %exchange.1 = (f32[512,4,8,128]{3,2,1,0:T(8,128)S(1)}, f32[2,2,4,4,32,128]{5,4,3,2,1,0:T(8,128)S(1)}, bf16[16,2,256,96]{3,2,1,0:T(8,128)(2,1)S(1)}, f32[8,32,256]{2,1,0:T(8,128)S(1)}) custom-call(bf16[2,8,2048]{2,1,0:T(8,128)(2,1)} %bitcast.13, bf16[2,8,2048]{2,1,0:T(8,128)(2,1)} %bitcast.14, bf16[4,2048]{1,0:T(4,128)(2,1)} %bitcast.15, ...), custom_call_target="tpu_custom_call" | custom-call | tf_op jit(solution)/shard_map/exchange/pallas_call | solution.py:570
  37.5 4.1 %finish.1 = (bf16[32,256]{1,0:T(8,128)(2,1)}, f32[512,4,8,128]{3,2,1,0:T(8,128)}) custom-call(f32[512,4,8,128]{3,2,1,0:T(8,128)S(1)} %get-tuple-element.6.held, f32[2,2,4,4,32,128]{5,4,3,2,1,0:T(8,128)S(1)} %get-tuple-element.7.delta_all, bf16[16,2,256,96]{3,2,1,0:T(8,128)(2,1)S(1)} %get-tuple-element.8.lift, f32[8,32,256]{2,1,0:T(8,128)S(1)} %get-tuple-element.9.outs_land), custom_call_target="tpu_custom_call" | custom-call | tf_op jit(solution)/shard_map/finish/pallas_call | solution.py:629

commit v5 on v4

v5 whole, which is shorter than its diff:
```python
import math

import jax
import jax.numpy as jnp
from jax import lax
from jax.experimental import pallas as pl
from jax.experimental.pallas import tpu as pltpu
from jax.sharding import PartitionSpec as P

F32 = jnp.float32
BF16 = jnp.bfloat16
NT = (((1,), (1,)), ((), ()))
SIDE = 4
COLS = 40
HEADS = 8


def softplus(x):
    return jnp.maximum(x, 0.0) + jnp.log1p(jnp.exp(-jnp.abs(x)))


def size(ref):
    return math.prod(ref.shape) * jnp.dtype(ref.dtype).itemsize


class Group:
    def __init__(self, copies, sem, like):
        self.copies, self.sem, self.like, self.bytes = copies, sem, like, 0

    def start(self, src, dst, peer):
        self.bytes += size(src)
        self.copies.sent[self.like is None].bytes += size(src)
        pltpu.make_async_remote_copy(
            src_ref=src,
            dst_ref=dst,
            send_sem=self.copies.sent[self.like is None].sem,
            recv_sem=self.sem,
            device_id=peer,
            device_id_type=pl.DeviceIdType.MESH,
        ).start()

    def wait(self):
        if self.like is None:
            rows = self.bytes // size(self.copies.held.at[0])
            ref = self.copies.held.at[pl.ds(0, rows)]
        else:
            ref = self.like.at[pl.ds(0, self.bytes // size(self.like.at[0]))]
        pltpu.make_async_copy(ref, ref, self.sem).wait()


class Copies:
    def __init__(self, held, little, send, recv):
        self.held, self.recv, self.used = held, recv, 0
        self.sent = {True: Group(self, send.at[0], None), False: Group(self, send.at[1], little)}

    def group(self, like=None):
        self.used += 1
        return Group(self, self.recv.at[self.used - 1], like)

    def drain(self):
        for group in self.sent.values():
            group.wait()


class Ring:
    def __init__(self, me, row_of):
        self.me = me
        self.right = lax.rem(me + 1, SIDE)
        self.far = lax.rem(me + 2, SIDE)
        self.left = lax.rem(me + 3, SIDE)
        self.to_right = {"row": row_of(self.right)}
        self.to_far = {"row": row_of(self.far)}
        self.to_left = {"row": row_of(self.left)}
        self.at = {"far": self.far, "right": self.right, "left": self.left}
        self.to = {"far": self.to_far, "right": self.to_right, "left": self.to_left}


class Scatter:
    def __init__(self, copies, ring, pieces, part, land, fine):
        self.ring, self.pieces, self.part, self.land = ring, pieces, part, land
        if fine:
            self.relay = [copies.group() for _ in pieces]
            self.joint = [copies.group() for _ in pieces]
        else:
            self.relay = [copies.group()] * len(pieces)
            self.joint = [copies.group()] * len(pieces)

    def send_far(self):
        r = self.ring
        for n, b in enumerate(self.pieces):
            for half, peer in ((0, r.to_left), (1, r.to_right)):
                self.relay[n].start(self.part(half, r.far).at[b], self.land.at[half, 0, b], peer)

    def send_right(self):
        r = self.ring
        self.joint[0].start(self.part(0, r.right), self.land.at[0, 1], r.to_right)

    def send_left(self):
        r = self.ring
        self.joint[0].start(self.part(1, r.left), self.land.at[1, 1], r.to_left)

    def forward(self):
        r = self.ring
        for n, b in enumerate(self.pieces):
            if self.relay[n] not in self.relay[:n]:
                self.relay[n].wait()
            for half, to, peer in ((0, r.left, r.to_left), (1, r.right, r.to_right)):
                piece = self.part(half, to).at[b]
                piece[...] = piece[...] + self.land[half, 0, b]
                self.joint[n].start(piece, self.land.at[half, 2, b], peer)

    def finish(self, n):
        b = self.pieces[n]
        if self.joint[n] not in self.joint[:n]:
            self.joint[n].wait()
        for half in (0, 1):
            piece = self.part(half, self.ring.me).at[b]
            piece[...] = piece[...] + self.land[half, 1, b] + self.land[half, 2, b]


WAYS = ("far", "right", "left")


def split(x):
    hi = x.astype(BF16)
    return hi, (x - hi.astype(F32)).astype(BF16)


def growth(delta_all, lift, o, first, second, r):
    hi, lo = split(jnp.concatenate([delta_all[o, c, first, second] for c in (0, 1)], axis=1))
    add = jnp.dot(lift[r, o], jnp.concatenate([hi, lo, hi], axis=0), preferred_element_type=F32)
    return [add[:, c * 128 : (c + 1) * 128].reshape(hi.shape[0], 8, 128) for c in (0, 1)]


def exchange_kernel(
    wq_hbm,
    wk_hbm,
    wd_hbm,
    wb_hbm,
    decay_log,
    dt_bias,
    gain,
    hid_hbm,
    wv_hbm,
    wz_hbm,
    w_out_hbm,
    state,
    held,
    delta_all,
    lift,
    outs_land,
    wq,
    wk,
    wd,
    wb,
    hid,
    wv,
    wz,
    w_out,
    proj,
    decay_all,
    part,
    land1,
    land2,
    small,
    small_land1,
    small_land2,
    scales,
    normed,
    outs,
    load_sem,
    weight_sem,
    send_sem,
    recv_sem,
):
    row = lax.axis_index("row")
    head = lax.axis_index("head")
    x, z = row // SIDE, lax.rem(row, SIDE)
    rows = SIDE * SIDE
    blk = held.shape[0] // rows

    barrier = pltpu.get_barrier_semaphore()
    peers = []
    for d in (1, 2, 3):
        peers.append({"row": lax.rem(x + d, SIDE) * SIDE + z})
        peers.append({"row": x * SIDE + lax.rem(z + d, SIDE)})
    for d in range(1, HEADS):
        peers.append({"head": lax.rem(head + d, HEADS)})
    for peer in peers:
        pl.semaphore_signal(barrier, inc=1, device_id=peer, device_id_type=pl.DeviceIdType.MESH)

    def row_at(o, first, second):
        return first * SIDE + second if o == 0 else second * SIDE + first

    rings1 = [
        Ring(x, lambda a: row_at(0, a, z)),
        Ring(z, lambda a: row_at(1, a, x)),
    ]
    rings2 = [
        Ring(z, lambda b: row_at(0, x, b)),
        Ring(x, lambda b: row_at(1, z, b)),
    ]
    order = [[r.far, r.right, r.left, r.me] for r in rings1]

    first = []
    small_weights = ((wq_hbm, wq), (wk_hbm, wk), (wd_hbm, wd), (wb_hbm, wb))
    quarter = hid.shape[0] // 4
    pieces = tuple((hid_hbm.at[pl.ds(n * quarter, quarter)], hid.at[pl.ds(n * quarter, quarter)]) for n in range(4))
    for n, (src, dst) in enumerate(small_weights):
        first.append(pltpu.make_async_copy(src, dst, weight_sem.at[n]))
        first[-1].start()
    for src, dst in pieces:
        pltpu.make_async_copy(src, dst, weight_sem.at[4]).start()
    all_hid = pltpu.make_async_copy(hid, hid, weight_sem.at[4])

    def load(j, o):
        for b in range(SIDE):
            at = row_at(o, order[o][j], b) * blk
            pltpu.make_async_copy(
                state.at[pl.ds(at, blk), pl.ds(2 * o, 2)],
                held.at[pl.ds(at, blk), pl.ds(2 * o, 2)],
                load_sem.at[j * 2 + o],
            ).start()

    def await_load(j, o):
        ref = held.at[pl.ds(0, SIDE * blk // 2)]
        pltpu.make_async_copy(ref, ref, load_sem.at[j * 2 + o]).wait()

    load(0, 0)

    proj[...] = jnp.zeros_like(proj)
    for copy in first:
        copy.wait()
    load(0, 1)
    w = jnp.concatenate(
        [
            wq[0].astype(F32),
            wq[1].astype(F32),
            wk[0].astype(F32),
            wk[1].astype(F32),
            wd[...].astype(F32),
            wb[...].astype(F32),
        ],
        axis=0,
    ).astype(BF16)
    all_hid.wait()
    for j in (1, 2, 3):
        for o in (0, 1):
            load(j, o)
    proj[:, :COLS] = lax.dot_general(hid[...], w, NT, preferred_element_type=F32)

    copies = Copies(held, small_land1, send_sem, recv_sem)
    lane = lax.broadcasted_iota(jnp.int32, (blk, 128), 1)
    own = [
        lane // 8 + n * 16 == lax.broadcasted_iota(jnp.int32, (blk, 128), 0) for n in range(8 * blk // 128)
    ]

    def spread(vec, base):
        wide = jnp.where(lane < 8, vec if base == 0 else pltpu.roll(vec, 128 - base, 1), 0.0)
        for shift in (8, 16, 32, 64):
            wide = wide + pltpu.roll(wide, shift, 1)
        return jnp.concatenate([jnp.where(m, wide, 0.0) for m in own], axis=1)

    def read_block(o, first, second):
        at = pl.multiple_of(row_at(o, first, second) * blk, blk)
        vec = proj[pl.ds(at, blk), :]
        wide = jnp.concatenate([spread(vec, 16 + 8 * o), spread(vec, 8 * o)], axis=0)
        wide = jnp.concatenate(split(wide), axis=0)
        hi, lo = split(
            jnp.concatenate([held[pl.ds(at, blk), 2 * o + c].reshape(8 * blk, 128) for c in (0, 1)], axis=1)
        )
        main = jnp.dot(wide, hi, preferred_element_type=F32)
        rest = jnp.dot(wide[: 2 * blk], lo, preferred_element_type=F32)
        read = main[: 2 * blk] + (main[2 * blk :] + rest)
        for c in (0, 1):
            for t in (0, 1):
                part[o, c, t, first, second] = read[t * blk : (t + 1) * blk, c * 128 : (c + 1) * 128]

    def send_sums():
        for a in range(SIDE):
            cols = proj[a * 128 : (a + 1) * 128, :].T
            terms = []
            for u, v in ((0, 0), (16, 16), (0, 16)):
                for hk in (0, 8):
                    product = cols[u + hk : u + hk + 8] * cols[v + hk : v + hk + 8]
                    terms.append(jnp.sum(product, axis=0, keepdims=True))
            terms.append(jnp.zeros((2, 128), F32))
            small[a] = jnp.concatenate(terms, axis=0)
        group = copies.group(small_land1)
        for n, name in enumerate(WAYS):
            group.start(small.at[rings1[0].at[name]], small_land1.at[n], rings1[0].to[name])
        return group

    def scatter1(o, t):
        r = rings2[o]
        pieces = (r.far, r.right, r.left, r.me)
        return Scatter(copies, rings1[o], pieces, lambda c, a: part.at[o, c, t, a], land1.at[o, t], t == 0)

    def own_piece(o, c, t):
        return part.at[o, c, t, rings1[o].me, rings2[o].me]

    def finish1(o, t, s):
        r = rings2[o]
        group = copies.group()
        for n, name in enumerate(WAYS):
            s.finish(n)
            group.start(part.at[o, :, t, rings1[o].me, r.at[name]], land2.at[o, t, n], r.to[name])
        return group

    def finish2(o, t, first, s):
        first.finish(3)
        s.wait()
        for c in (0, 1):
            piece = own_piece(o, c, t)
            piece[...] = piece[...] + land2[o, t, 0, c] + land2[o, t, 1, c] + land2[o, t, 2, c]

    k1 = [scatter1(o, 0) for o in (0, 1)]
    q1 = [scatter1(o, 1) for o in (0, 1)]

    for j in range(SIDE):
        for o in (0, 1):
            await_load(j, o)
            if j == 0:
                for b in range(SIDE):
                    read_block(o, order[o][j], b)
                if o == 0:
                    pl.semaphore_wait(barrier, len(peers))
                k1[o].send_far()
        if j == 0:
            small1 = send_sums()
            for o in (0, 1):
                q1[o].send_far()
        else:
            for o in (0, 1):
                for b in range(SIDE):
                    read_block(o, order[o][j], b)
        if j == 1:
            for o in (0, 1):
                k1[o].send_right()
            load_weights = []
            for n, (src, dst) in enumerate(((wv_hbm, wv), (wz_hbm, wz), (w_out_hbm, w_out))):
                load_weights.append(pltpu.make_async_copy(src, dst, weight_sem.at[n + 5]))
                load_weights[-1].start()
        if j == 2:
            for o in (0, 1):
                k1[o].send_left()
    for s in k1:
        s.forward()
    for s in q1:
        s.send_right()
        s.send_left()
    small1.wait()
    small[x] = small[x] + small_land1[0] + small_land1[1] + small_land1[2]
    small2 = copies.group(small_land2)
    for n, name in enumerate(WAYS):
        small2.start(small.at[x], small_land2.at[n], rings2[0].to[name])

    mine = pl.ds(pl.multiple_of(row * blk, blk), blk)
    own_hid = hid[mine, :]
    chunks = own_hid.shape[1] // 256
    tall = jnp.concatenate([own_hid[:, n * 256 : (n + 1) * 256] for n in range(chunks)], axis=0)
    repeat = (
        lax.broadcasted_iota(jnp.int32, (256, 1024), 1) // 4 == lax.broadcasted_iota(jnp.int32, (256, 1024), 0)
    ).astype(F32).astype(BF16)
    tall = jnp.dot(tall, repeat, preferred_element_type=F32)
    at_head = lax.broadcasted_iota(jnp.int32, (blk, 1024), 1) % 4
    load_weights[0].wait()
    load_weights[1].wait()
    both = jnp.zeros((4 * blk, 256), F32)
    for n in range(chunks):
        piece = tall[n * blk : (n + 1) * blk]
        piece = jnp.concatenate([jnp.where(at_head == h, piece, 0.0).astype(BF16) for h in range(4)], axis=0)
        at = slice(n * 1024, (n + 1) * 1024)
        weights = jnp.concatenate([wv[at, :], wz[at, :]], axis=1)
        both = both + jnp.dot(piece, weights, preferred_element_type=F32)

    for s in q1:
        s.forward()
    k2 = [finish1(o, 0, k1[o]) for o in (0, 1)]

    decay_all[...] = jnp.exp(-jnp.exp(decay_log[...]) * softplus(proj[:, 32:36] + dt_bias[...]))
    own_t = lax.broadcasted_iota(jnp.int32, (8 * blk, 3 * blk), 0) // 8 == lax.rem(
        lax.broadcasted_iota(jnp.int32, (8 * blk, 3 * blk), 1), blk
    )
    picks = [
        (
            lax.broadcasted_iota(jnp.int32, (8 * blk, COLS), 1)
            == 16 + 8 * o + lax.broadcasted_iota(jnp.int32, (8 * blk, COLS), 0) % 8
        )
        .astype(F32)
        .astype(BF16)
        for o in (0, 1)
    ]

    def prepare(r, carry):
        at = pl.ds(pl.multiple_of(r * blk, blk), blk)
        hi, lo = split(proj[at, :COLS])
        three = jnp.concatenate([hi.astype(F32), hi.astype(F32), lo.astype(F32)], axis=0).astype(BF16)
        decay = decay_all[at, :]
        for o in (0, 1):
            wide = lax.dot_general(picks[o], three, NT, preferred_element_type=F32)
            lift[r, o] = jnp.where(own_t, wide, 0.0).astype(BF16)
            for c in (0, 1):
                h = 2 * o + c
                keep = jnp.broadcast_to(decay[:, h : h + 1], (blk, 128))
                held[at, h] = keep[:, None, :] * held[at, h]
        return carry

    lax.fori_loop(0, rows // 2, prepare, 0)

    q2 = [finish1(o, 1, q1[o]) for o in (0, 1)]

    small2.wait()
    total = small[x] + small_land2[0] + small_land2[1] + small_land2[2]
    scales[...] = jnp.concatenate([total, jnp.zeros((120, 128), F32)], axis=0).T
    raw = scales[pl.ds(pl.multiple_of(z * blk, blk), blk), :]
    q_scale = lax.rsqrt(1.0 + raw[:, 0:2])
    k_scale = lax.rsqrt(1.0 + raw[:, 2:4])
    unit_dot = raw[:, 4:6] * q_scale * k_scale
    decay = decay_all[mine, :]
    beta = 1.0 / (1.0 + jnp.exp(-proj[mine, 36:40]))

    g2 = {(o, name): copies.group() for o in (0, 1) for name in WAYS}
    near = {(o, name): copies.group() for o in (0, 1) for name in ("me", "left", "right", "far")}
    onward = [copies.group() for _ in (0, 1)]
    straight = [copies.group() for _ in (0, 1)]

    def send_near(o, name):
        r = rings1[o]
        b = rings2[o].me if name == "me" else rings2[o].at[name]
        piece = delta_all.at[o, :, r.me, b]
        for way in ("right", "left"):
            near[o, name].start(piece, piece, r.to[way])
        if name == "far":
            straight[o].start(piece, piece, r.to_far)

    def send_on(o, name):
        r = rings1[o]
        b = rings2[o].me if name == "me" else rings2[o].at[name]
        near[o, name].wait()
        for half, at, peer in ((0, r.left, r.to_right), (1, r.right, r.to_left)):
            piece = delta_all.at[o, half, at, b]
            onward[o].start(piece, piece, peer)

    deltas = []
    for o in (0, 1):
        finish2(o, 0, k1[o], k2[o])
        for c in (0, 1):
            h = 2 * o + c
            readk = own_piece(o, c, 0)[...] * k_scale[:, o : o + 1]
            value = both[h * blk : (h + 1) * blk, :128]
            delta = beta[:, h : h + 1] * (value - decay[:, h : h + 1] * readk)
            delta_all[o, c, rings1[o].me, rings2[o].me] = delta * k_scale[:, o : o + 1]
            deltas.append(delta)
        here = delta_all.at[o, :, rings1[o].me, rings2[o].me]
        for name in ("right", "left", "far"):
            g2[o, name].start(here, here, rings2[o].to[name])
    for o in (0, 1):
        send_near(o, "me")

    lax.fori_loop(rows // 2, rows, prepare, 0)
    for o in (0, 1):
        for sent, name in (("right", "left"), ("left", "right")):
            g2[o, sent].wait()
            send_near(o, name)
    for o in (0, 1):
        finish2(o, 1, q1[o], q2[o])
        for c in (0, 1):
            h = 2 * o + c
            old = own_piece(o, c, 1)[...] * q_scale[:, o : o + 1]
            readq = decay[:, h : h + 1] * old + unit_dot[:, o : o + 1] * deltas[h]
            meansq = jnp.mean(readq * readq, axis=-1, keepdims=True)
            gate = both[h * blk : (h + 1) * blk, 128:]
            gate = gate / (1.0 + jnp.exp(-gate))
            normed[:, h * 128 : (h + 1) * 128] = (readq * lax.rsqrt(meansq + 0.5) * gain[...] * gate).astype(BF16)

    load_weights[2].wait()
    width = outs.shape[-1]
    for n in range(HEADS):
        outs[n] = jnp.dot(normed[...], w_out[:, n * width : (n + 1) * width], preferred_element_type=F32)
    out_group = copies.group()
    for d in range(1, HEADS):
        to = lax.rem(head + d, HEADS)
        out_group.start(outs.at[to], outs_land.at[head], {"head": to})
    outs_land[head] = outs[head]

    for o in (0, 1):
        send_on(o, "me")
        g2[o, "far"].wait()
        send_near(o, "far")
    for o in (0, 1):
        for name in ("left", "right"):
            send_on(o, name)

    def update_rows(o, first):
        for b in range(SIDE):
            r = row_at(o, first, b)
            at = pl.ds(pl.multiple_of(r * blk, blk), blk)
            add = growth(delta_all, lift, o, first, b, r)
            for c in (0, 1):
                h = 2 * o + c
                held[at, h] = held[at, h] + add[c]

    for o in (0, 1):
        update_rows(o, rings1[o].me)
    for o in (0, 1):
        near[o, "far"].wait()
    for o in (0, 1):
        update_rows(o, rings1[o].left)
        update_rows(o, rings1[o].right)
    out_group.wait()
    for o in (0, 1):
        onward[o].wait()
        straight[o].wait()
    copies.drain()


def finish_kernel(held, delta_all, lift, outs_land, layer_out, new_state, last, layer, sems):
    row = lax.axis_index("row")
    spots = (row // SIDE, lax.rem(row, SIDE))
    blk = held.shape[0] // (SIDE * SIDE)

    def store(src, o, r, count=1):
        dst = new_state.at[pl.ds(pl.multiple_of(r * blk, blk), count * blk), pl.ds(2 * o, 2)]
        pltpu.make_async_copy(src, dst, sems.at[0]).start()

    for d in (0, 1, 3):
        first = lax.rem(spots[0] + d, SIDE)
        at = pl.ds(pl.multiple_of(first * SIDE * blk, blk), SIDE * blk)
        store(held.at[at, pl.ds(0, 2)], 0, first * SIDE, SIDE)
        for b in range(SIDE):
            r = b * SIDE + lax.rem(spots[1] + d, SIDE)
            store(held.at[pl.ds(pl.multiple_of(r * blk, blk), blk), pl.ds(2, 2)], 1, r)
    total = outs_land[0]
    for n in range(1, HEADS):
        total = total + outs_land[n]
    layer[...] = total.astype(BF16)
    layer_copy = pltpu.make_async_copy(layer, layer_out, sems.at[1])
    layer_copy.start()
    for o in (0, 1):
        first = lax.rem(spots[o] + 2, SIDE)
        for b in range(SIDE):
            r = first * SIDE + b if o == 0 else b * SIDE + first
            at = pl.ds(pl.multiple_of(r * blk, blk), blk)
            add = growth(delta_all, lift, o, first, b, r)
            for c in (0, 1):
                last[o * SIDE + b, :, c] = held[at, 2 * o + c] + add[c]
            store(last.at[o * SIDE + b], o, r)
    layer_copy.wait()
    pltpu.make_async_copy(held, new_state, sems.at[0]).wait()


def local(
    hidden_in,
    w_query,
    w_key,
    w_value,
    w_zgate,
    w_decay,
    w_beta,
    decay_log,
    dt_bias,
    norm_gain,
    w_out,
    state,
):
    seqs, width = hidden_in.shape
    rows = SIDE * SIDE
    blk = seqs // rows
    vmem = pl.BlockSpec(memory_space=pltpu.VMEM)
    anywhere = pl.BlockSpec(memory_space=pltpu.HBM)
    held, delta_all, lift, outs_land = pl.pallas_call(
        exchange_kernel,
        out_shape=(
            pltpu.VMEM(state.shape, F32),
            pltpu.VMEM((2, 2, SIDE, SIDE, blk, 128), F32),
            pltpu.VMEM((rows, 2, 8 * blk, 3 * blk), BF16),
            pltpu.VMEM((HEADS, blk, 256), F32),
        ),
        in_specs=[anywhere] * 4 + [vmem] * 3 + [anywhere] * 5,
        out_specs=(vmem,) * 4,
        scratch_shapes=[
            pltpu.VMEM((2, 8, width), BF16),
            pltpu.VMEM((2, 8, width), BF16),
            pltpu.VMEM((4, width), BF16),
            pltpu.VMEM((4, width), BF16),
            pltpu.VMEM((seqs, width), BF16),
            pltpu.VMEM((4 * width, 128), BF16),
            pltpu.VMEM((4 * width, 128), BF16),
            pltpu.VMEM((512, width), BF16),
            pltpu.VMEM((seqs, 128), F32),
            pltpu.VMEM((seqs, 4), F32),
            pltpu.VMEM((2, 2, 2, SIDE, SIDE, blk, 128), F32),
            pltpu.VMEM((2, 2, 2, 3, SIDE, blk, 128), F32),
            pltpu.VMEM((2, 2, 3, 2, blk, 128), F32),
            pltpu.VMEM((SIDE, 8, 128), F32),
            pltpu.VMEM((6, 8, 128), F32),
            pltpu.VMEM((3, 8, 128), F32),
            pltpu.VMEM((128, 128), F32),
            pltpu.VMEM((blk, 512), BF16),
            pltpu.VMEM((HEADS, blk, 256), F32),
            pltpu.SemaphoreType.DMA((2 * SIDE,)),
            pltpu.SemaphoreType.DMA((8,)),
            pltpu.SemaphoreType.DMA((2,)),
            pltpu.SemaphoreType.DMA((45,)),
        ],
        compiler_params=pltpu.CompilerParams(
            collective_id=0, has_side_effects=True, vmem_limit_bytes=36 * 1024 * 1024
        ),
        name="exchange",
    )(
        *(
            pltpu.with_memory_space_constraint(operand, pltpu.HBM)
            for operand in (
                jnp.transpose(w_query, (1, 2, 0)),
                jnp.transpose(w_key, (1, 2, 0)),
                jnp.transpose(w_decay, (1, 0)),
                jnp.transpose(w_beta, (1, 0)),
                decay_log.reshape(1, 4),
                dt_bias.reshape(1, 4),
                norm_gain.reshape(1, 128),
                hidden_in,
                w_value.reshape(4 * width, 128),
                w_zgate.reshape(4 * width, 128),
                w_out.reshape(512, width),
                state,
            )
        )
    )
    layer_out, new_state = pl.pallas_call(
        finish_kernel,
        out_shape=(
            jax.ShapeDtypeStruct((blk, 256), BF16),
            jax.ShapeDtypeStruct(state.shape, F32),
        ),
        in_specs=[vmem] * 4,
        out_specs=(anywhere, anywhere),
        scratch_shapes=[
            pltpu.VMEM((2 * SIDE, blk, 2, 8, 128), F32),
            pltpu.VMEM((blk, 256), BF16),
            pltpu.SemaphoreType.DMA((2,)),
        ],
        compiler_params=pltpu.CompilerParams(vmem_limit_bytes=16 * 1024 * 1024),
        name="finish",
    )(*(pltpu.with_memory_space_constraint(a, pltpu.VMEM) for a in (held, delta_all, lift, outs_land)))
    return layer_out, new_state


def solution(mesh):
    in_specs = (
        P(),
        P(None, "head", "row"),
        P(None, "head", "row"),
        P(None, "head", None),
        P(None, "head", None),
        P(None, "head"),
        P(None, "head"),
        P("head"),
        P("head"),
        P(),
        P("head", None, None),
        P(None, "head", "row", None),
    )
    out_specs = (P("row", "head"), P(None, "head", "row", None))
    return jax.shard_map(local, mesh=mesh, in_specs=in_specs, out_specs=out_specs, check_vma=False)
```

time: 41.7 us -> 37.9 us (0.909); the launches traced: 41.6 us -> 37.3 us
  Pallas kernels: 41 us -> 36.7 us
    pallas_call x1, Pallas kernels: 36.9 us -> 33.4 us  [local(): pl.pallas_call(exchange_kernel, out_shape=(pltpu.VMEM(state.shape, F32),...]
    pallas_call x1, Pallas kernels: 4.1 us -> 3.3 us  [local(): pl.pallas_call(finish_kernel, out_shape=(jax.ShapeDtypeStruct((blk, 256),...]
where the time goes in v5:
time: 37.9 us; the launch traced here: 37.3 us
  Pallas kernels  36.7 us (97%)
  between operations  0.64 us (2%)
    pallas_call x1, Pallas kernels, local(): pl.pallas_call(exchange_kernel, out_shape=(pltpu.VMEM(state.shape, F32),...  33.4 us
    pallas_call x1, Pallas kernels, local(): pl.pallas_call(finish_kernel, out_shape=(jax.ShapeDtypeStruct((blk, 256),...  3.3 us

profile of v5, /device:TPU:0, one launch (start us, length us, event | category | flops | bytes accessed | tf_op | source)
XLA Modules:
  0.0 37.3 jit_solution(5728269944728623359)
XLA Ops:
  0.6 33.4 %exchange.1 = (f32[512,4,8,128]{3,2,1,0:T(8,128)S(1)}, f32[2,2,4,4,32,128]{5,4,3,2,1,0:T(8,128)S(1)}, bf16[16,2,256,96]{3,2,1,0:T(8,128)(2,1)S(1)}, f32[8,32,256]{2,1,0:T(8,128)S(1)}) custom-call(bf16[2,8,2048]{2,1,0:T(8,128)(2,1)} %bitcast.13, bf16[2,8,2048]{2,1,0:T(8,128)(2,1)} %bitcast.14, bf16[4,2048]{1,0:T(4,128)(2,1)} %bitcast.15, ...), custom_call_target="tpu_custom_call" | custom-call | tf_op jit(solution)/shard_map/exchange/pallas_call | solution.py:572
  34.0 3.3 %finish.1 = (bf16[32,256]{1,0:T(8,128)(2,1)}, f32[512,4,8,128]{3,2,1,0:T(8,128)}) custom-call(f32[512,4,8,128]{3,2,1,0:T(8,128)S(1)} %get-tuple-element.6.held, f32[2,2,4,4,32,128]{5,4,3,2,1,0:T(8,128)S(1)} %get-tuple-element.7.delta_all, bf16[16,2,256,96]{3,2,1,0:T(8,128)(2,1)S(1)} %get-tuple-element.8.lift, f32[8,32,256]{2,1,0:T(8,128)S(1)} %get-tuple-element.9.outs_land), custom_call_target="tpu_custom_call" | custom-call | tf_op jit(solution)/shard_map/finish/pallas_call | solution.py:630

commit v6 on v5

--- a/solution.py
+++ b/solution.py
@@ -13,6 +13,7 @@
 SIDE = 4
 COLS = 40
 HEADS = 8
+PITCH = 40
 
 
 def softplus(x):
@@ -41,8 +42,8 @@
 
     def wait(self):
         if self.like is None:
-            rows = self.bytes // size(self.copies.held.at[0])
-            ref = self.copies.held.at[pl.ds(0, rows)]
+            rows = self.bytes // size(self.copies.held.at[0, pl.ds(0, 4)])
+            ref = self.copies.held.at[pl.ds(0, rows), pl.ds(0, 4)]
         else:
             ref = self.like.at[pl.ds(0, self.bytes // size(self.like.at[0]))]
         pltpu.make_async_copy(ref, ref, self.sem).wait()
@@ -179,6 +180,20 @@
     rows = SIDE * SIDE
     blk = held.shape[0] // rows
 
+    def row_at(o, first, second):
+        return first * SIDE + second if o == 0 else second * SIDE + first
+
+    first = []
+    small_weights = ((wq_hbm, wq), (wk_hbm, wk), (wd_hbm, wd), (wb_hbm, wb))
+    quarter = hid.shape[0] // 4
+    pieces = tuple((hid_hbm.at[pl.ds(n * quarter, quarter)], hid.at[pl.ds(n * quarter, quarter)]) for n in range(4))
+    for src, dst in pieces:
+        pltpu.make_async_copy(src, dst, weight_sem.at[4]).start()
+    for n, (src, dst) in enumerate(small_weights):
+        first.append(pltpu.make_async_copy(src, dst, weight_sem.at[n]))
+        first[-1].start()
+    all_hid = pltpu.make_async_copy(hid, hid, weight_sem.at[4])
+
     barrier = pltpu.get_barrier_semaphore()
     peers = []
     for d in (1, 2, 3):
@@ -189,9 +204,6 @@
     for peer in peers:
         pl.semaphore_signal(barrier, inc=1, device_id=peer, device_id_type=pl.DeviceIdType.MESH)
 
-    def row_at(o, first, second):
-        return first * SIDE + second if o == 0 else second * SIDE + first
-
     rings1 = [
         Ring(x, lambda a: row_at(0, a, z)),
         Ring(z, lambda a: row_at(1, a, x)),
@@ -202,17 +214,6 @@
     ]
     order = [[r.far, r.right, r.left, r.me] for r in rings1]
 
-    first = []
-    small_weights = ((wq_hbm, wq), (wk_hbm, wk), (wd_hbm, wd), (wb_hbm, wb))
-    quarter = hid.shape[0] // 4
-    pieces = tuple((hid_hbm.at[pl.ds(n * quarter, quarter)], hid.at[pl.ds(n * quarter, quarter)]) for n in range(4))
-    for n, (src, dst) in enumerate(small_weights):
-        first.append(pltpu.make_async_copy(src, dst, weight_sem.at[n]))
-        first[-1].start()
-    for src, dst in pieces:
-        pltpu.make_async_copy(src, dst, weight_sem.at[4]).start()
-    all_hid = pltpu.make_async_copy(hid, hid, weight_sem.at[4])
-
     def load(j, o):
         for b in range(SIDE):
             at = row_at(o, order[o][j], b) * blk
@@ -223,15 +224,13 @@
             ).start()
 
     def await_load(j, o):
-        ref = held.at[pl.ds(0, SIDE * blk // 2)]
+        ref = held.at[pl.ds(0, SIDE * blk // 2), pl.ds(0, 4)]
         pltpu.make_async_copy(ref, ref, load_sem.at[j * 2 + o]).wait()
-
-    load(0, 0)
 
     proj[...] = jnp.zeros_like(proj)
     for copy in first:
         copy.wait()
-    load(0, 1)
+    load(0, 0)
     w = jnp.concatenate(
         [
             wq[0].astype(F32),
@@ -244,37 +243,31 @@
         axis=0,
     ).astype(BF16)
     all_hid.wait()
+    load(0, 1)
     for j in (1, 2, 3):
         for o in (0, 1):
             load(j, o)
     proj[:, :COLS] = lax.dot_general(hid[...], w, NT, preferred_element_type=F32)
 
     copies = Copies(held, small_land1, send_sem, recv_sem)
-    lane = lax.broadcasted_iota(jnp.int32, (blk, 128), 1)
-    own = [
-        lane // 8 + n * 16 == lax.broadcasted_iota(jnp.int32, (blk, 128), 0) for n in range(8 * blk // 128)
-    ]
-
-    def spread(vec, base):
-        wide = jnp.where(lane < 8, vec if base == 0 else pltpu.roll(vec, 128 - base, 1), 0.0)
-        for shift in (8, 16, 32, 64):
-            wide = wide + pltpu.roll(wide, shift, 1)
-        return jnp.concatenate([jnp.where(m, wide, 0.0) for m in own], axis=1)
+    flat = held.reshape(held.shape[0] * PITCH, 128)
 
     def read_block(o, first, second):
         at = pl.multiple_of(row_at(o, first, second) * blk, blk)
-        vec = proj[pl.ds(at, blk), :]
-        wide = jnp.concatenate([spread(vec, 16 + 8 * o), spread(vec, 8 * o)], axis=0)
-        wide = jnp.concatenate(split(wide), axis=0)
-        hi, lo = split(
-            jnp.concatenate([held[pl.ds(at, blk), 2 * o + c].reshape(8 * blk, 128) for c in (0, 1)], axis=1)
-        )
-        main = jnp.dot(wide, hi, preferred_element_type=F32)
-        rest = jnp.dot(wide[: 2 * blk], lo, preferred_element_type=F32)
-        read = main[: 2 * blk] + (main[2 * blk :] + rest)
-        for c in (0, 1):
-            for t in (0, 1):
-                part[o, c, t, first, second] = read[t * blk : (t + 1) * blk, c * 128 : (c + 1) * 128]
+        for g in range(blk // 8):
+            vec = proj[pl.ds(at + g * 8, 8), :]
+            sums = [[None, None], [None, None]]
+            for i in range(8):
+                for c in (0, 1):
+                    start = (at + g * 8) * PITCH + (2 * o + c) * 8 + i
+                    values = flat[pl.ds(start, 8, stride=PITCH), :]
+                    for t, base in ((0, 16), (1, 0)):
+                        n = base + 8 * o + i
+                        term = jnp.broadcast_to(vec[:, n : n + 1], (8, 128)) * values
+                        sums[t][c] = term if i == 0 else sums[t][c] + term
+            for c in (0, 1):
+                for t in (0, 1):
+                    part[o, c, t, first, second, g * 8 : (g + 1) * 8] = sums[t][c]
 
     def send_sums():
         for a in range(SIDE):
@@ -400,10 +393,9 @@
         for o in (0, 1):
             wide = lax.dot_general(picks[o], three, NT, preferred_element_type=F32)
             lift[r, o] = jnp.where(own_t, wide, 0.0).astype(BF16)
-            for c in (0, 1):
-                h = 2 * o + c
-                keep = jnp.broadcast_to(decay[:, h : h + 1], (blk, 128))
-                held[at, h] = keep[:, None, :] * held[at, h]
+            pair = held[at, pl.ds(2 * o, 2)]
+            keep = [jnp.broadcast_to(decay[:, h : h + 1], (blk, 128))[:, None, :] for h in (2 * o, 2 * o + 1)]
+            held[at, pl.ds(2 * o, 2)] = jnp.stack([keep[c] * pair[:, c] for c in (0, 1)], axis=1)
         return carry
 
     lax.fori_loop(0, rows // 2, prepare, 0)
@@ -497,9 +489,8 @@
             r = row_at(o, first, b)
             at = pl.ds(pl.multiple_of(r * blk, blk), blk)
             add = growth(delta_all, lift, o, first, b, r)
-            for c in (0, 1):
-                h = 2 * o + c
-                held[at, h] = held[at, h] + add[c]
+            pair = held[at, pl.ds(2 * o, 2)]
+            held[at, pl.ds(2 * o, 2)] = jnp.stack([pair[:, c] + add[c] for c in (0, 1)], axis=1)
 
     for o in (0, 1):
         update_rows(o, rings1[o].me)
@@ -543,11 +534,11 @@
             r = first * SIDE + b if o == 0 else b * SIDE + first
             at = pl.ds(pl.multiple_of(r * blk, blk), blk)
             add = growth(delta_all, lift, o, first, b, r)
-            for c in (0, 1):
-                last[o * SIDE + b, :, c] = held[at, 2 * o + c] + add[c]
+            pair = held[at, pl.ds(2 * o, 2)]
+            last[o * SIDE + b] = jnp.stack([pair[:, c] + add[c] for c in (0, 1)], axis=1)
             store(last.at[o * SIDE + b], o, r)
     layer_copy.wait()
-    pltpu.make_async_copy(held, new_state, sems.at[0]).wait()
+    pltpu.make_async_copy(new_state, new_state, sems.at[0]).wait()
 
 
 def local(
@@ -572,7 +563,7 @@
     held, delta_all, lift, outs_land = pl.pallas_call(
         exchange_kernel,
         out_shape=(
-            pltpu.VMEM(state.shape, F32),
+            pltpu.VMEM((seqs, PITCH // 8, 8, 128), F32),
             pltpu.VMEM((2, 2, SIDE, SIDE, blk, 128), F32),
             pltpu.VMEM((rows, 2, 8 * blk, 3 * blk), BF16),
             pltpu.VMEM((HEADS, blk, 256), F32),

time: 37.9 us -> 37.8 us (level)
  no operation moved by 1% of the time
where the time goes in v6:
time: 37.8 us; the launch traced here: 37.2 us
  Pallas kernels  36.5 us (97%)
  between operations  0.64 us (2%)
    pallas_call x1, Pallas kernels, local(): pl.pallas_call(exchange_kernel, out_shape=(pltpu.VMEM((seqs, PITCH // 8,...  33.2 us
    pallas_call x1, Pallas kernels, local(): pl.pallas_call(finish_kernel, out_shape=(jax.ShapeDtypeStruct((blk, 256),...  3.31 us

profile of v6, /device:TPU:0, one launch (start us, length us, event | category | flops | bytes accessed | tf_op | source)
XLA Modules:
  0.0 37.2 jit_solution(12636782498206284473)
XLA Ops:
  0.6 33.2 %exchange.1 = (f32[512,5,8,128]{3,2,1,0:T(8,128)S(1)}, f32[2,2,4,4,32,128]{5,4,3,2,1,0:T(8,128)S(1)}, bf16[16,2,256,96]{3,2,1,0:T(8,128)(2,1)S(1)}, f32[8,32,256]{2,1,0:T(8,128)S(1)}) custom-call(bf16[2,8,2048]{2,1,0:T(8,128)(2,1)} %bitcast.13, bf16[2,8,2048]{2,1,0:T(8,128)(2,1)} %bitcast.14, bf16[4,2048]{1,0:T(4,128)(2,1)} %bitcast.15, ...), custom_call_target="tpu_custom_call" | custom-call | tf_op jit(solution)/shard_map/exchange/pallas_call | solution.py:563
  33.8 3.3 %finish.1 = (bf16[32,256]{1,0:T(8,128)(2,1)}, f32[512,4,8,128]{3,2,1,0:T(8,128)}) custom-call(f32[512,5,8,128]{3,2,1,0:T(8,128)S(1)} %get-tuple-element.6.held, f32[2,2,4,4,32,128]{5,4,3,2,1,0:T(8,128)S(1)} %get-tuple-element.7.delta_all, bf16[16,2,256,96]{3,2,1,0:T(8,128)(2,1)S(1)} %get-tuple-element.8.lift, f32[8,32,256]{2,1,0:T(8,128)S(1)} %get-tuple-element.9.outs_land), custom_call_target="tpu_custom_call" | custom-call | tf_op jit(solution)/shard_map/finish/pallas_call | solution.py:621

commit v7 on v6

--- a/solution.py
+++ b/solution.py
@@ -28,9 +28,10 @@
     def __init__(self, copies, sem, like):
         self.copies, self.sem, self.like, self.bytes = copies, sem, like, 0
 
-    def start(self, src, dst, peer):
-        self.bytes += size(src)
-        self.copies.sent[self.like is None].bytes += size(src)
+    def start(self, src, dst, peer, count=True):
+        if count:
+            self.bytes += size(src)
+            self.copies.sent[self.like is None].bytes += size(src)
         pltpu.make_async_remote_copy(
             src_ref=src,
             dst_ref=dst,
@@ -79,18 +80,14 @@
 class Scatter:
     def __init__(self, copies, ring, pieces, part, land, fine):
         self.ring, self.pieces, self.part, self.land = ring, pieces, part, land
-        if fine:
-            self.relay = [copies.group() for _ in pieces]
-            self.joint = [copies.group() for _ in pieces]
-        else:
-            self.relay = [copies.group()] * len(pieces)
-            self.joint = [copies.group()] * len(pieces)
-
-    def send_far(self):
+        self.relay = [copies.group() for _ in pieces] if fine else [copies.group()] * len(pieces)
+        self.joint = [copies.group() for _ in pieces]
+
+    def send_far(self, count=True):
         r = self.ring
         for n, b in enumerate(self.pieces):
             for half, peer in ((0, r.to_left), (1, r.to_right)):
-                self.relay[n].start(self.part(half, r.far).at[b], self.land.at[half, 0, b], peer)
+                self.relay[n].start(self.part(half, r.far).at[b], self.land.at[half, 0, b], peer, count)
 
     def send_right(self):
         r = self.ring
@@ -138,9 +135,9 @@
     wk_hbm,
     wd_hbm,
     wb_hbm,
-    decay_log,
-    dt_bias,
-    gain,
+    decay_log_hbm,
+    dt_bias_hbm,
+    gain_hbm,
     hid_hbm,
     wv_hbm,
     wz_hbm,
@@ -154,6 +151,9 @@
     wk,
     wd,
     wb,
+    decay_log,
+    dt_bias,
+    gain,
     hid,
     wv,
     wz,
@@ -192,6 +192,10 @@
     for n, (src, dst) in enumerate(small_weights):
         first.append(pltpu.make_async_copy(src, dst, weight_sem.at[n]))
         first[-1].start()
+    params = []
+    for n, (src, dst) in enumerate(((decay_log_hbm, decay_log), (dt_bias_hbm, dt_bias), (gain_hbm, gain))):
+        params.append(pltpu.make_async_copy(src, dst, weight_sem.at[8 + n]))
+        params[-1].start()
     all_hid = pltpu.make_async_copy(hid, hid, weight_sem.at[4])
 
     barrier = pltpu.get_barrier_semaphore()
@@ -244,10 +248,14 @@
     ).astype(BF16)
     all_hid.wait()
     load(0, 1)
+    half = hid.shape[1] // 2
+    proj[:, :COLS] = sum(
+        lax.dot_general(hid[:, at], w[:, at], NT, preferred_element_type=F32)
+        for at in (slice(0, half), slice(half, 2 * half))
+    )
     for j in (1, 2, 3):
         for o in (0, 1):
             load(j, o)
-    proj[:, :COLS] = lax.dot_general(hid[...], w, NT, preferred_element_type=F32)
 
     copies = Copies(held, small_land1, send_sem, recv_sem)
     flat = held.reshape(held.shape[0] * PITCH, 128)
@@ -292,13 +300,14 @@
     def own_piece(o, c, t):
         return part.at[o, c, t, rings1[o].me, rings2[o].me]
 
-    def finish1(o, t, s):
-        r = rings2[o]
-        group = copies.group()
+    def finish1(t, scatters):
+        groups = [copies.group() for _ in scatters]
         for n, name in enumerate(WAYS):
-            s.finish(n)
-            group.start(part.at[o, :, t, rings1[o].me, r.at[name]], land2.at[o, t, n], r.to[name])
-        return group
+            for o, s in enumerate(scatters):
+                r = rings2[o]
+                s.finish(n)
+                groups[o].start(part.at[o, :, t, rings1[o].me, r.at[name]], land2.at[o, t, n], r.to[name])
+        return groups
 
     def finish2(o, t, first, s):
         first.finish(3)
@@ -321,8 +330,12 @@
                 k1[o].send_far()
         if j == 0:
             small1 = send_sums()
-            for o in (0, 1):
-                q1[o].send_far()
+
+            @pl.when(lax.rem(head, 2) == 0)
+            def _():
+                for o in (0, 1):
+                    q1[o].send_far()
+
         else:
             for o in (0, 1):
                 for b in range(SIDE):
@@ -339,6 +352,12 @@
                 k1[o].send_left()
     for s in k1:
         s.forward()
+
+    @pl.when(lax.rem(head, 2) == 1)
+    def _():
+        for o in (0, 1):
+            q1[o].send_far(count=False)
+
     for s in q1:
         s.send_right()
         s.send_left()
@@ -369,8 +388,10 @@
 
     for s in q1:
         s.forward()
-    k2 = [finish1(o, 0, k1[o]) for o in (0, 1)]
-
+    k2 = finish1(0, k1)
+
+    for copy in params:
+        copy.wait()
     decay_all[...] = jnp.exp(-jnp.exp(decay_log[...]) * softplus(proj[:, 32:36] + dt_bias[...]))
     own_t = lax.broadcasted_iota(jnp.int32, (8 * blk, 3 * blk), 0) // 8 == lax.rem(
         lax.broadcasted_iota(jnp.int32, (8 * blk, 3 * blk), 1), blk
@@ -400,7 +421,7 @@
 
     lax.fori_loop(0, rows // 2, prepare, 0)
 
-    q2 = [finish1(o, 1, q1[o]) for o in (0, 1)]
+    q2 = finish1(1, q1)
 
     small2.wait()
     total = small[x] + small_land2[0] + small_land2[1] + small_land2[2]
@@ -452,10 +473,6 @@
 
     lax.fori_loop(rows // 2, rows, prepare, 0)
     for o in (0, 1):
-        for sent, name in (("right", "left"), ("left", "right")):
-            g2[o, sent].wait()
-            send_near(o, name)
-    for o in (0, 1):
         finish2(o, 1, q1[o], q2[o])
         for c in (0, 1):
             h = 2 * o + c
@@ -468,14 +485,30 @@
 
     load_weights[2].wait()
     width = outs.shape[-1]
-    for n in range(HEADS):
-        outs[n] = jnp.dot(normed[...], w_out[:, n * width : (n + 1) * width], preferred_element_type=F32)
     out_group = copies.group()
-    for d in range(1, HEADS):
-        to = lax.rem(head + d, HEADS)
-        out_group.start(outs.at[to], outs_land.at[head], {"head": to})
-    outs_land[head] = outs[head]
-
+    chip, core = head // 2, lax.rem(head, 2)
+    order_out = []
+    for up, other in ((2, 0), (2, 1), (1, 0), (1, 1), (3, 0), (3, 1), (0, 1), (0, 0)):
+        order_out.append(lax.rem(chip + up, HEADS // 2) * 2 + lax.rem(core + other, 2))
+    for some in ((0, 1, 2, 3), (4, 5, 6, 7)):
+        pieces = []
+        for n in some:
+            at = pl.ds(pl.multiple_of(order_out[n] * width, width), width)
+            pieces.append(jnp.dot(normed[...], w_out[:, at], preferred_element_type=F32))
+        for n, piece in zip(some, pieces):
+            if n == 7:
+                outs_land[head] = piece
+            else:
+                outs[n] = piece
+        for n in some:
+            if n == 7:
+                continue
+            out_group.start(outs.at[n], outs_land.at[head], {"head": order_out[n]})
+
+    for o in (0, 1):
+        for sent, name in (("right", "left"), ("left", "right")):
+            g2[o, sent].wait()
+            send_near(o, name)
     for o in (0, 1):
         send_on(o, "me")
         g2[o, "far"].wait()
@@ -568,13 +601,16 @@
             pltpu.VMEM((rows, 2, 8 * blk, 3 * blk), BF16),
             pltpu.VMEM((HEADS, blk, 256), F32),
         ),
-        in_specs=[anywhere] * 4 + [vmem] * 3 + [anywhere] * 5,
+        in_specs=[anywhere] * 12,
         out_specs=(vmem,) * 4,
         scratch_shapes=[
             pltpu.VMEM((2, 8, width), BF16),
             pltpu.VMEM((2, 8, width), BF16),
             pltpu.VMEM((4, width), BF16),
             pltpu.VMEM((4, width), BF16),
+            pltpu.VMEM((1, 4), F32),
+            pltpu.VMEM((1, 4), F32),
+            pltpu.VMEM((1, 128), F32),
             pltpu.VMEM((seqs, width), BF16),
             pltpu.VMEM((4 * width, 128), BF16),
             pltpu.VMEM((4 * width, 128), BF16),
@@ -591,9 +627,9 @@
             pltpu.VMEM((blk, 512), BF16),
             pltpu.VMEM((HEADS, blk, 256), F32),
             pltpu.SemaphoreType.DMA((2 * SIDE,)),
-            pltpu.SemaphoreType.DMA((8,)),
+            pltpu.SemaphoreType.DMA((11,)),
             pltpu.SemaphoreType.DMA((2,)),
-            pltpu.SemaphoreType.DMA((45,)),
+            pltpu.SemaphoreType.DMA((51,)),
         ],
         compiler_params=pltpu.CompilerParams(
             collective_id=0, has_side_effects=True, vmem_limit_bytes=36 * 1024 * 1024

time: 37.8 us -> 37 us (0.979)
  Pallas kernels: 36.5 us -> 36 us
    pallas_call x1, Pallas kernels: 33.2 us -> 32.6 us  [local(): pl.pallas_call(exchange_kernel, out_shape=(pltpu.VMEM((seqs, PITCH // 8,...]
where the time goes in v7:
time: 37 us; the launch traced here: 36.6 us
  Pallas kernels  36 us (97%)
  between operations  0.64 us (2%)
    pallas_call x1, Pallas kernels, local(): pl.pallas_call(exchange_kernel, out_shape=(pltpu.VMEM((seqs, PITCH // 8,...  32.6 us
    pallas_call x1, Pallas kernels, local(): pl.pallas_call(finish_kernel, out_shape=(jax.ShapeDtypeStruct((blk, 256),...  3.31 us

profile of v7, /device:TPU:0, one launch (start us, length us, event | category | flops | bytes accessed | tf_op | source)
XLA Modules:
  0.0 36.6 jit_solution(5301613703896680405)
XLA Ops:
  0.6 32.6 %exchange.1 = (f32[512,5,8,128]{3,2,1,0:T(8,128)S(1)}, f32[2,2,4,4,32,128]{5,4,3,2,1,0:T(8,128)S(1)}, bf16[16,2,256,96]{3,2,1,0:T(8,128)(2,1)S(1)}, f32[8,32,256]{2,1,0:T(8,128)S(1)}) custom-call(bf16[2,8,2048]{2,1,0:T(8,128)(2,1)} %bitcast.13, bf16[2,8,2048]{2,1,0:T(8,128)(2,1)} %bitcast.14, bf16[4,2048]{1,0:T(4,128)(2,1)} %bitcast.15, ...), custom_call_target="tpu_custom_call" | custom-call | tf_op jit(solution)/shard_map/exchange/pallas_call | solution.py:596
  33.3 3.3 %finish.1 = (bf16[32,256]{1,0:T(8,128)(2,1)}, f32[512,4,8,128]{3,2,1,0:T(8,128)}) custom-call(f32[512,5,8,128]{3,2,1,0:T(8,128)S(1)} %get-tuple-element.6.held, f32[2,2,4,4,32,128]{5,4,3,2,1,0:T(8,128)S(1)} %get-tuple-element.7.delta_all, bf16[16,2,256,96]{3,2,1,0:T(8,128)(2,1)S(1)} %get-tuple-element.8.lift, f32[8,32,256]{2,1,0:T(8,128)S(1)} %get-tuple-element.9.outs_land), custom_call_target="tpu_custom_call" | custom-call | tf_op jit(solution)/shard_map/finish/pallas_call | solution.py:657

commit v8 on v7

--- a/solution.py
+++ b/solution.py
@@ -169,6 +169,8 @@
     scales,
     normed,
     outs,
+    picked,
+    wide,
     load_sem,
     weight_sem,
     send_sem,
@@ -232,27 +234,24 @@
         pltpu.make_async_copy(ref, ref, load_sem.at[j * 2 + o]).wait()
 
     proj[...] = jnp.zeros_like(proj)
+    for o in (0, 1):
+        source = lax.broadcasted_iota(jnp.int32, (128, 1024), 0) % 64
+        picked[o] = (source == 8 * o + lax.broadcasted_iota(jnp.int32, (128, 1024), 1) // 128).astype(F32).astype(BF16)
     for copy in first:
         copy.wait()
     load(0, 0)
-    w = jnp.concatenate(
-        [
-            wq[0].astype(F32),
-            wq[1].astype(F32),
-            wk[0].astype(F32),
-            wk[1].astype(F32),
-            wd[...].astype(F32),
-            wb[...].astype(F32),
-        ],
-        axis=0,
-    ).astype(BF16)
+    parts = [ref[n].astype(F32) for ref in (wq, wk) for n in (0, 1)] + [wd[...].astype(F32), wb[...].astype(F32)]
+    w = jnp.concatenate(parts, axis=0).astype(BF16)
+    swapped = jnp.concatenate(parts[2:4] + parts[:2] + parts[4:], axis=0).astype(BF16)
     all_hid.wait()
     load(0, 1)
-    half = hid.shape[1] // 2
-    proj[:, :COLS] = sum(
-        lax.dot_general(hid[:, at], w[:, at], NT, preferred_element_type=F32)
-        for at in (slice(0, half), slice(half, 2 * half))
-    )
+    half = hid.shape[0] // 2
+    upper = lax.dot_general(hid[:half, :], w, NT, preferred_element_type=F32)
+    lower = lax.dot_general(hid[half:, :], swapped, NT, preferred_element_type=F32)
+    proj[:half, :COLS] = upper
+    proj[half:, 0:16] = lower[:, 16:32]
+    proj[half:, 16:32] = lower[:, 0:16]
+    proj[half:, 32:COLS] = lower[:, 32:COLS]
     for j in (1, 2, 3):
         for o in (0, 1):
             load(j, o)
@@ -260,22 +259,29 @@
     copies = Copies(held, small_land1, send_sem, recv_sem)
     flat = held.reshape(held.shape[0] * PITCH, 128)
 
-    def read_block(o, first, second):
-        at = pl.multiple_of(row_at(o, first, second) * blk, blk)
-        for g in range(blk // 8):
-            vec = proj[pl.ds(at + g * 8, 8), :]
-            sums = [[None, None], [None, None]]
-            for i in range(8):
+    def read_blocks(o, first):
+        starts = [pl.multiple_of(row_at(o, first, b) * blk, blk) for b in range(SIDE)]
+        vecs = [proj[pl.ds(at, blk), :] for at in starts]
+        hi, lo = split(jnp.concatenate(vecs, axis=0))
+        both_terms = (hi.astype(F32) + pltpu.roll(lo.astype(F32), 64, 1)).astype(BF16)
+        wide[...] = jnp.dot(both_terms, picked[o], preferred_element_type=F32)
+        for b, at in enumerate(starts):
+            for g in range(blk // 8):
+                mine = slice(g * 8, (g + 1) * 8)
+                sums = [[None, None], [None, None]]
+                for i in range(8):
+                    n = 16 + 8 * o + i
+                    key = jnp.broadcast_to(vecs[b][mine, n : n + 1], (8, 128))
+                    query = wide[b * blk + g * 8 : b * blk + (g + 1) * 8, i * 128 : (i + 1) * 128]
+                    for c in (0, 1):
+                        start = (at + g * 8) * PITCH + (2 * o + c) * 8 + i
+                        values = flat[pl.ds(start, 8, stride=PITCH), :]
+                        for t, vector in ((0, key), (1, query)):
+                            term = vector * values
+                            sums[t][c] = term if i == 0 else sums[t][c] + term
                 for c in (0, 1):
-                    start = (at + g * 8) * PITCH + (2 * o + c) * 8 + i
-                    values = flat[pl.ds(start, 8, stride=PITCH), :]
-                    for t, base in ((0, 16), (1, 0)):
-                        n = base + 8 * o + i
-                        term = jnp.broadcast_to(vec[:, n : n + 1], (8, 128)) * values
-                        sums[t][c] = term if i == 0 else sums[t][c] + term
-            for c in (0, 1):
-                for t in (0, 1):
-                    part[o, c, t, first, second, g * 8 : (g + 1) * 8] = sums[t][c]
+                    for t in (0, 1):
+                        part[o, c, t, first, b, mine] = sums[t][c]
 
     def send_sums():
         for a in range(SIDE):
@@ -323,8 +329,7 @@
         for o in (0, 1):
             await_load(j, o)
             if j == 0:
-                for b in range(SIDE):
-                    read_block(o, order[o][j], b)
+                read_blocks(o, order[o][j])
                 if o == 0:
                     pl.semaphore_wait(barrier, len(peers))
                 k1[o].send_far()
@@ -338,8 +343,7 @@
 
         else:
             for o in (0, 1):
-                for b in range(SIDE):
-                    read_block(o, order[o][j], b)
+                read_blocks(o, order[o][j])
         if j == 1:
             for o in (0, 1):
                 k1[o].send_right()
@@ -626,6 +630,8 @@
             pltpu.VMEM((128, 128), F32),
             pltpu.VMEM((blk, 512), BF16),
             pltpu.VMEM((HEADS, blk, 256), F32),
+            pltpu.VMEM((2, 128, 1024), BF16),
+            pltpu.VMEM((SIDE * blk, 1024), F32),
             pltpu.SemaphoreType.DMA((2 * SIDE,)),
             pltpu.SemaphoreType.DMA((11,)),
             pltpu.SemaphoreType.DMA((2,)),

time: 37 us -> 37.9 us (1.024)
  Pallas kernels: 36 us -> 37.1 us
    pallas_call x1, Pallas kernels: 32.6 us -> 33.8 us  [local(): pl.pallas_call(exchange_kernel, out_shape=(pltpu.VMEM((seqs, PITCH // 8,...]
where the time goes in v8:
time: 37.9 us; the launch traced here: 37.7 us
  Pallas kernels  37.1 us (98%)
  between operations  0.64 us (2%)
    pallas_call x1, Pallas kernels, local(): pl.pallas_call(exchange_kernel, out_shape=(pltpu.VMEM((seqs, PITCH // 8,...  33.8 us
    pallas_call x1, Pallas kernels, local(): pl.pallas_call(finish_kernel, out_shape=(jax.ShapeDtypeStruct((blk, 256),...  3.31 us

profile of v8, /device:TPU:0, one launch (start us, length us, event | category | flops | bytes accessed | tf_op | source)
XLA Modules:
  0.0 37.7 jit_solution(3261610753802473733)
XLA Ops:
  0.6 33.8 %exchange.1 = (f32[512,5,8,128]{3,2,1,0:T(8,128)S(1)}, f32[2,2,4,4,32,128]{5,4,3,2,1,0:T(8,128)S(1)}, bf16[16,2,256,96]{3,2,1,0:T(8,128)(2,1)S(1)}, f32[8,32,256]{2,1,0:T(8,128)S(1)}) custom-call(bf16[2,8,2048]{2,1,0:T(8,128)(2,1)} %bitcast.13, bf16[2,8,2048]{2,1,0:T(8,128)(2,1)} %bitcast.14, bf16[4,2048]{1,0:T(4,128)(2,1)} %bitcast.15, ...), custom_call_target="tpu_custom_call" | custom-call | tf_op jit(solution)/shard_map/exchange/pallas_call | solution.py:600
  34.4 3.3 %finish.1 = (bf16[32,256]{1,0:T(8,128)(2,1)}, f32[512,4,8,128]{3,2,1,0:T(8,128)}) custom-call(f32[512,5,8,128]{3,2,1,0:T(8,128)S(1)} %get-tuple-element.6.held, f32[2,2,4,4,32,128]{5,4,3,2,1,0:T(8,128)S(1)} %get-tuple-element.7.delta_all, bf16[16,2,256,96]{3,2,1,0:T(8,128)(2,1)S(1)} %get-tuple-element.8.lift, f32[8,32,256]{2,1,0:T(8,128)S(1)} %get-tuple-element.9.outs_land), custom_call_target="tpu_custom_call" | custom-call | tf_op jit(solution)/shard_map/finish/pallas_call | solution.py:663
